TPU v7x, 32 devices: a whole 2x2x4 slice. The times are simulated.
32 devices in a mesh: px: 4 (over y, x), py: 8 (over z, core).
Axes of the slice: x: 2, y: 2, z: 4, core: 2. Of those that a mesh axis runs over, the one named last changes fastest.
Arguments:
- white_noise: float32 [2, 64, 256, 256], P(None, 'px', 'py'), may hold values from -6 to 6
- spectrum: float32 [64, 256, 256], P('px', 'py'), may hold values from 0.1 to 2, as said below
- group_table: int32 [3, 8], replicated, may hold values from 0 to 7, each once within a row
Outputs:
- modulus: float32 [2, 64, 256, 256], P(None, 'px', 'py')
- level_one: float32 [2, 32, 128, 128], P(None, 'px', 'py')
- level_two: float32 [2, 16, 64, 64], P(None, 'px', 'py')
- level_three: float32 [2, 8, 32, 32], P(None, 'px', 'py')
Inputs may be any that keep to these rules, and one draw needn't show every extreme that they name: spectrum[j, m, k] equals spectrum[(64 - j) % 64, (256 - m) % 256, (256 - k) % 256]. `group_table`: each row is a permutation of 0 to 7.
All inputs are finite; a program needn't handle non-finite values.
Results may differ from a plain program's by a relative error of at most 0.000088.
Values sent between devices are 32-bit elements; how exact they have to be, the bound alone decides.
A program may use at most 192 MiB of HBM per device.

v0:
```python
import numpy as np

import jax
import jax.numpy as jnp
from jax import lax
from jax.experimental import pallas as pl
from jax.experimental.pallas import tpu as pltpu
from jax.sharding import PartitionSpec as P


def angles_of(length):
    positions = np.arange(length, dtype=np.int64)
    return (positions[:, None] * positions[None, :] % length) * (2.0 * np.pi / length)


def complex_array(length, direction):
    angles = angles_of(length)
    cos, sin = np.cos(angles), direction * np.sin(angles)
    return np.stack([np.stack([cos, sin], 1), np.stack([-sin, cos], 1)], 0)


def complex_table(length, direction):
    return jnp.asarray(complex_array(length, direction), jnp.float32)


def half_tables(length):
    angles = angles_of(length)[:, : length // 2]
    ahead = np.stack([np.cos(angles), -np.sin(angles)], 1)
    back = 2.0 * ahead
    nyquist = np.where(np.arange(length) % 2 == 0, 1.0, -1.0)
    ahead[:, 1, 0] = nyquist
    back[:, 0, 0] = 1.0
    back[:, 1, 0] = nyquist
    return jnp.asarray(ahead, jnp.float32), jnp.asarray(back, jnp.float32)


def einsum(pattern, left, right):
    return jnp.einsum(pattern, left, right, precision=lax.Precision.HIGH)


def swap_first(values):
    first = values[:, :, :1]
    turned = jnp.swapaxes(first, 0, 1)
    return jnp.concatenate([turned, values[:, :, 1:]], 2)


def coarsen(values):
    members, size_x, size_y, size_z = values.shape
    blocks = values.reshape(members, size_x // 2, 2, size_y // 2, 2, size_z // 2, 2)
    return blocks.mean(axis=(2, 4, 6))


def general_path(white_noise, spectrum, group_table):
    members, cells_x, cells_y, length_z = white_noise.shape
    size_px, size_py = lax.axis_size("px"), lax.axis_size("py")
    length_x, length_y = cells_x * size_px, cells_y * size_py
    half_z = length_z // 2
    block_py, block = half_z // size_py, half_z // size_py // size_px
    z_ahead, z_back = half_tables(length_z)
    scale = 1.0 / (length_x * length_y * length_z)

    table = jnp.transpose(spectrum, (2, 0, 1))
    last = jnp.broadcast_to(table[half_z : half_z + 1], (size_py, 1, cells_x, cells_y))
    table = jnp.concatenate([table[:half_z].reshape(size_py, block_py, cells_x, cells_y), last], 1)
    table = lax.all_to_all(table, "py", split_axis=0, concat_axis=3, tiled=True)[0]
    last = jnp.broadcast_to(table[block_py:], (size_px, 1, cells_x, length_y))
    table = jnp.concatenate([table[:block_py].reshape(size_px, block, cells_x, length_y), last], 1)
    table = lax.all_to_all(table, "px", split_axis=0, concat_axis=2, tiled=True)[0] * scale
    is_first = (lax.axis_index("px") == 0) & (lax.axis_index("py") == 0)
    other = jnp.where(is_first, table[block:], table[:1])
    tables = jnp.stack([table[:block], jnp.concatenate([other, table[1:block]], 0)], 0)

    values = einsum("fxyz,zck->fckxy", white_noise, z_ahead)
    values = swap_first(values)
    values = lax.all_to_all(values, "py", split_axis=2, concat_axis=4, tiled=True)
    values = einsum("fckxy,cydm->fdkxm", values, complex_table(length_y, -1.0))
    values = lax.all_to_all(values, "px", split_axis=2, concat_axis=3, tiled=True)
    values = einsum("fckxm,cxdj->fdkjm", values, complex_table(length_x, -1.0))
    values = values * tables[:, None]
    values = einsum("fckjm,cjdx->fdkxm", values, complex_table(length_x, 1.0))
    values = lax.all_to_all(values, "px", split_axis=3, concat_axis=2, tiled=True)
    values = einsum("fckxm,cmdy->fdkxy", values, complex_table(length_y, 1.0))
    values = lax.all_to_all(values, "py", split_axis=4, concat_axis=2, tiled=True)
    values = swap_first(values)
    fields = einsum("fckxy,zck->fxyz", values, z_back)
    modulus = jnp.exp(0.5 * fields)

    levels = []
    level = modulus
    for _ in range(3):
        level = coarsen(level)
        levels.append(level)
    pieces = [jnp.reshape(level, (size_py, -1)) for level in levels]
    widths = [piece.shape[1] for piece in pieces]
    joined = jnp.concatenate(pieces, 1)
    spread = lax.all_to_all(joined, "py", split_axis=0, concat_axis=0, tiled=True)
    picked, start = [], 0
    for index, width in enumerate(widths):
        part = spread[:, start : start + width]
        picked.append(jnp.take(part, group_table[index], axis=0))
        start += width
    joined = lax.all_to_all(
        jnp.concatenate(picked, 1), "py", split_axis=0, concat_axis=0, tiled=True
    )
    routed, start = [], 0
    for level, width in zip(levels, widths):
        routed.append(joined[:, start : start + width].reshape(level.shape))
        start += width
    return (modulus, routed[0], routed[1], routed[2])


LANES = 128
MESH = pl.DeviceIdType.MESH


def dot(left, right):
    return jnp.dot(
        left, right, precision=lax.Precision.HIGHEST, preferred_element_type=jnp.float32
    )


def lane_of(shape):
    return lax.broadcasted_iota(jnp.int32, shape, len(shape) - 1)


def exchange(arrays, width):
    arrays = list(arrays)
    lane = lane_of(arrays[0].shape)
    distance = 1
    while distance < len(arrays):
        step = distance * width
        low = (lane // step) % 2 == 0
        for index in range(len(arrays)):
            if (index // distance) % 2 == 0:
                first, second = arrays[index], arrays[index + distance]
                arrays[index] = jnp.where(low, first, pltpu.roll(second, step, 1))
                arrays[index + distance] = jnp.where(
                    low, pltpu.roll(first, LANES - step, 1), second
                )
        distance *= 2
    return arrays


def swap_slot(first, second):
    at_zero = lane_of(first.shape) == 0
    return jnp.where(at_zero, second, first), jnp.where(at_zero, first, second)


def z_forward_kernel(sizes, noise_ref, spectrum_ref, table_ref, out_ref, held):
    lo, hi, kept = sizes
    cells_y = noise_ref.shape[2]
    for f in range(2):
        rows = noise_ref[f].reshape(lo * hi * cells_y, noise_ref.shape[3])
        held[f] = dot(rows, table_ref[...])

    def tile(f, c, x):
        return held[f, pl.ds(x * cells_y, cells_y), pl.ds(c * LANES, LANES)]

    for xh in range(hi):
        tiles = {}
        for xl in range(lo):
            x = xh * lo + xl
            mixed = swap_slot(tile(0, 1, x), tile(1, 0, x))
            members = ((tile(0, 0, x), mixed[0]), (mixed[1], tile(1, 1, x)))
            for f in range(2):
                for c in range(2):
                    tiles[f, c, xl] = members[f][c]
        for f in range(2):
            for c in range(2):
                moved = exchange([tiles[f, c, xl] for xl in range(lo)], kept)
                for p in range(lo):
                    out_ref[p, (f * 2 + c) * hi + xh] = moved[p]
    group = lane_of((cells_y, LANES))
    last = jnp.zeros((cells_y, LANES), jnp.float32)
    for xh in range(hi):
        names = [xh * lo + xl for xl in range(lo)]
        moved = exchange([spectrum_ref[x, :, pl.ds(0, LANES)] for x in names], kept)
        for p in range(lo):
            out_ref[p, 4 * hi + xh] = moved[p]
        for xl in range(lo):
            value = spectrum_ref[names[xl], :, pl.ds(LANES, 1)]
            last = jnp.where(group == xl * kept + xh, value, last)
    for p in range(lo):
        out_ref[p, 5 * hi] = last


def y_forward_kernel(sizes, in_ref, table_ref, out_ref):
    lo, hi, kept = sizes
    length_y = table_ref.shape[1]
    ranks = 2 * hi
    half = length_y // 2

    def whole(t):
        return in_ref[:, t].reshape(length_y, LANES)

    for f in range(2):
        arrays = [None] * ranks
        for xh in range(hi):
            pair = [whole((f * 2 + c) * hi + xh) for c in range(2)]
            product = dot(table_ref[...], jnp.concatenate(pair, 1))
            by_cos, by_sin = product[:length_y], product[length_y:]
            arrays[xh] = by_cos[:, :LANES] + by_sin[:, LANES:]
            arrays[hi + xh] = by_cos[:, LANES:] - by_sin[:, :LANES]
        moved = exchange(arrays, kept // ranks)
        for r in range(ranks):
            out_ref[r, pl.ds(f * length_y, length_y)] = moved[r]
    halves = []
    for mh in range(2):
        for xh in range(hi):
            halves.append(whole(4 * hi + xh)[mh * half : (mh + 1) * half])
    moved = exchange(halves, kept // ranks)
    last = whole(5 * hi)
    packed = last[:half] + pltpu.roll(last[half:], hi, 1)
    for r in range(ranks):
        out_ref[r, pl.ds(2 * length_y, half)] = moved[r]
        out_ref[r, pl.ds(2 * length_y + half, half)] = packed


def x_kernel(sizes, first_ref, in_ref, ahead_ref, back_ref, out_ref):
    lo, hi, kept = sizes
    ranks = 2 * hi
    length_y = out_ref.shape[1] // 2
    half = length_y // 2
    lane = lane_of((half, LANES))
    low = (lane // (hi * ranks)) % 2 == 0
    parts = [in_ref[r, pl.ds(2 * length_y, half)] for r in range(ranks)]
    tables = []
    for part in exchange(parts, 1):
        upper = jnp.where(low, part, pltpu.roll(part, hi * ranks, 1))
        lower = jnp.where(low, pltpu.roll(part, LANES - hi * ranks, 1), part)
        tables.append(jnp.concatenate([upper, lower], 0))
    last = [in_ref[r, pl.ds(2 * length_y + half, half)] for r in range(ranks)]
    last = jnp.concatenate(last, 1)
    source = lax.broadcasted_iota(jnp.int32, (ranks * LANES, LANES), 0)
    target = lax.broadcasted_iota(jnp.int32, (ranks * LANES, LANES), 1)
    same = (source // LANES == target % ranks) & ((source % LANES) // kept == target // kept)
    level = (target // ranks) % hi
    picked = []
    for mh in range(2):
        chosen = same & (source % kept == mh * hi + level)
        picked.append(dot(last, chosen.astype(jnp.float32)))
    last = jnp.concatenate(picked, 0)
    is_first = lax.broadcasted_iota(jnp.int32, last.shape, 0) * 0 + first_ref[0] == 1
    other = jnp.where(is_first, last, tables[0])
    for f in range(2):
        rows = pl.ds(f * length_y, length_y)
        arrays = exchange([in_ref[r, rows] for r in range(ranks)], 1)
        for q in range(ranks):
            table = other if f == 1 and q == 0 else tables[q]
            arrays[q] = dot(dot(arrays[q], ahead_ref[...]) * table, back_ref[...])
        arrays = exchange(arrays, 1)
        for r in range(ranks):
            out_ref[r, rows] = arrays[r]


def y_back_kernel(sizes, in_ref, table_ref, out_ref):
    lo, hi, kept = sizes
    ranks = 2 * hi
    length_y = table_ref.shape[1]
    cells_y = length_y // lo
    for f in range(2):
        rows = pl.ds(f * length_y, length_y)
        arrays = exchange([in_ref[r, rows] for r in range(ranks)], kept // ranks)
        for xh in range(hi):
            product = dot(table_ref[...], jnp.concatenate([arrays[xh], arrays[hi + xh]], 1))
            by_cos, by_sin = product[:length_y], product[length_y:]
            real = by_cos[:, :LANES] - by_sin[:, LANES:]
            imag = by_cos[:, LANES:] + by_sin[:, :LANES]
            out_ref[:, (f * 2) * hi + xh] = real.reshape(lo, cells_y, LANES)
            out_ref[:, (f * 2 + 1) * hi + xh] = imag.reshape(lo, cells_y, LANES)


def pool_matrix(rows, columns, weight, transposed):
    long_axis = 0 if transposed else 1
    shape = (columns, rows) if transposed else (rows, columns)
    long = lax.broadcasted_iota(jnp.int32, shape, long_axis)
    short = lax.broadcasted_iota(jnp.int32, shape, 1 - long_axis)
    return jnp.where(long // 2 == short, weight, 0.0).astype(jnp.float32)


def pool_rows(cells_x, cells_y):
    shape = (cells_x * cells_y // 4, cells_x * cells_y)
    short = lax.broadcasted_iota(jnp.int32, shape, 0)
    long = lax.broadcasted_iota(jnp.int32, shape, 1)
    same_x = long // (2 * cells_y) == short // (cells_y // 2)
    same_y = (long % cells_y) // 2 == short % (cells_y // 2)
    return jnp.where(same_x & same_y, 0.125, 0.0).astype(jnp.float32)


def z_back_kernel(sizes, in_ref, table_ref, modulus_ref, coarse_ref, held):
    lo, hi, kept = sizes
    cells_y = in_ref.shape[2]
    cells_x = lo * hi
    length_z = table_ref.shape[0]
    for xh in range(hi):
        tiles = {}
        for f in range(2):
            for c in range(2):
                arrays = [in_ref[p, (f * 2 + c) * hi + xh] for p in range(lo)]
                tiles[f, c] = exchange(arrays, kept)
        for xl in range(lo):
            mixed = swap_slot(tiles[0, 1][xl], tiles[1, 0][xl])
            members = ((tiles[0, 0][xl], mixed[0]), (mixed[1], tiles[1, 1][xl]))
            rows = pl.ds((xh * lo + xl) * cells_y, cells_y)
            for f in range(2):
                for c in range(2):
                    held[f, rows, pl.ds(c * LANES, LANES)] = members[f][c]
    coarse_ref[...] = jnp.zeros(coarse_ref.shape, jnp.float32)
    for f in range(2):
        values = jnp.exp(0.5 * dot(held[f], table_ref[...]))
        modulus_ref[f] = values.reshape(cells_x, cells_y, length_z)
        size_x, size_y, size_z = cells_x, cells_y, length_z
        start = 0
        for _ in range(3):
            right = pool_matrix(size_z // 2, size_z, 1.0, True)
            values = dot(pool_rows(size_x, size_y), dot(values, right))
            size_x, size_y, size_z = size_x // 2, size_y // 2, size_z // 2
            height = 2 * size_x * size_y // lo
            for d in range(lo // 2):
                piece = values[d * height : (d + 1) * height]
                place = (f * lo // 2 + d, pl.ds(start, height), pl.ds(0, size_z))
                coarse_ref[place] = piece
            start += height


def pick_kernel(heights, table_ref, in_ref, out_ref):
    for column in range(in_ref.shape[0]):
        start = 0
        for index, height in enumerate(heights):
            rows = pl.ds(start, height)
            out_ref[column, rows] = in_ref[table_ref[index, column], rows]
            start += height


def spread_kernel(axis, tail, used, in_ref, out_ref, own_sem, sends, recvs, tail_sends, tail_recvs):
    count, height = in_ref.shape[0], in_ref.shape[1]
    me = lax.axis_index(axis)
    used = used()
    rest = pl.ds(tail, height - tail)
    barrier = pltpu.get_barrier_semaphore()
    for away in range(1, count):
        peer = lax.rem(me + away, count)
        pl.semaphore_signal(barrier, inc=1, device_id={axis: peer}, device_id_type=MESH)
    own = pltpu.make_async_copy(in_ref.at[me], out_ref.at[me], own_sem)
    own.start()
    pl.semaphore_wait(barrier, count - 1)
    copies, extras = [], []
    for away in range(1, count):
        peer = lax.rem(me + away, count)
        copy = pltpu.make_async_remote_copy(
            src_ref=in_ref.at[peer, pl.ds(0, tail)],
            dst_ref=out_ref.at[me, pl.ds(0, tail)],
            send_sem=sends.at[away],
            recv_sem=recvs.at[away],
            device_id={axis: peer},
            device_id_type=MESH,
        )
        copy.start()
        copies.append(copy)
    for source in range(1, count):
        extra = pltpu.make_async_remote_copy(
            src_ref=in_ref.at[0, rest],
            dst_ref=out_ref.at[source, rest],
            send_sem=tail_sends.at[source],
            recv_sem=tail_recvs.at[source],
            device_id={axis: 0},
            device_id_type=MESH,
        )
        pl.when((me == source) & used)(extra.start)
        extras.append(extra)
    for source in range(count):

        @pl.when((me != source) & jnp.logical_not((me == 0) & used))
        def _():
            out_ref[source, rest] = jnp.zeros(out_ref.shape[1:], jnp.float32)[tail:]

    own.wait()
    for copy in copies:
        copy.wait()
    for source in range(1, count):
        pl.when((me == source) & used)(extras[source - 1].wait_send)
        pl.when((me == 0) & used)(extras[source - 1].wait_recv)


def spread_call(values, axis, number, tail, used):
    count = values.shape[0]

    def body(*refs):
        spread_kernel(axis, tail, used, *refs)

    return pl.pallas_call(
        body,
        out_shape=jax.ShapeDtypeStruct(values.shape, values.dtype),
        in_specs=[pl.BlockSpec(memory_space=pltpu.VMEM)],
        out_specs=pl.BlockSpec(memory_space=pltpu.VMEM),
        scratch_shapes=[pltpu.SemaphoreType.DMA] + [pltpu.SemaphoreType.DMA((count,))] * 4,
        compiler_params=pltpu.CompilerParams(collective_id=number, has_side_effects=True),
    )(values)


def spread(values, axis):
    return lax.all_to_all(values, axis, split_axis=0, concat_axis=0, tiled=True)


def lanes_path(white_noise, spectrum, group_table):
    members, cells_x, cells_y, length_z = white_noise.shape
    size_px, size_py = lax.axis_size("px"), lax.axis_size("py")
    length_x, length_y = cells_x * size_px, cells_y * size_py
    lo, hi = size_py, cells_x // size_py
    kept = LANES // size_py
    sizes = (lo, hi, kept)
    f32 = jnp.float32
    params = pltpu.CompilerParams(vmem_limit_bytes=48 * 1024 * 1024)

    def call(body, shapes, *operands, scratch=(), scalars=0):
        out = [jax.ShapeDtypeStruct(shape, f32) for shape in shapes]
        specs = [pl.BlockSpec(memory_space=pltpu.SMEM)] * scalars
        specs += [pl.BlockSpec(memory_space=pltpu.VMEM)] * (len(operands) - scalars)
        return pl.pallas_call(
            body,
            out_shape=out,
            in_specs=specs,
            out_specs=[pl.BlockSpec(memory_space=pltpu.VMEM)] * len(out),
            scratch_shapes=list(scratch),
            compiler_params=params,
        )(*operands)

    z_ahead, z_back = half_tables(length_z)
    z_ahead = z_ahead.reshape(length_z, length_z)
    z_back = z_back.reshape(length_z, length_z).T * (1.0 / (length_x * length_y * length_z))
    angles = angles_of(length_y)
    y_table = jnp.asarray(np.concatenate([np.cos(angles), np.sin(angles)], 0), f32)
    lane = np.arange(LANES)
    part = (lane // (hi * size_px)) % 2
    place = (lane % size_px) * cells_x + (lane // size_px % hi) * lo + lane // kept

    def x_table(direction):
        table = complex_array(length_x, direction)
        rows = table[part, place]
        return jnp.asarray(rows[:, part, place], f32)

    first = (lax.axis_index("px") == 0) & (lax.axis_index("py") == 0)
    first = first.astype(jnp.int32).reshape(1)
    held = pltpu.VMEM((members, cells_x * cells_y, length_z), f32)

    def bind(body):
        def bound(*refs):
            body(sizes, *refs)

        return bound

    tiles = 4 * hi
    (values,) = call(
        bind(z_forward_kernel),
        [(size_py, tiles + hi + 1, cells_y, LANES)],
        white_noise,
        spectrum,
        z_ahead,
        scratch=[held],
    )
    values = spread_call(values, "py", 0, tiles + hi, lambda: True)
    (values,) = call(
        bind(y_forward_kernel), [(size_px, 3 * length_y, LANES)], values, y_table
    )
    values = spread_call(
        values, "px", 1, 2 * length_y + length_y // 2, lambda: lax.axis_index("py") == 0
    )
    (values,) = call(
        bind(x_kernel),
        [(size_px, 2 * length_y, LANES)],
        first,
        values,
        x_table(-1.0),
        x_table(1.0),
        scalars=1,
    )
    values = spread(values, "px")
    (values,) = call(
        bind(y_back_kernel), [(size_py, tiles, cells_y, LANES)], values, y_table
    )
    values = spread(values, "py")
    shapes = []
    heights = []
    size = (cells_x, cells_y, length_z)
    for _ in range(3):
        size = tuple(extent // 2 for extent in size)
        shapes.append((members,) + size)
        heights.append(members * size[0] * size[1] // size_py)
    modulus, coarse = call(
        bind(z_back_kernel),
        [white_noise.shape, (size_py, sum(heights), LANES)],
        values,
        z_back,
        scratch=[held],
    )
    coarse = spread(coarse, "py")

    def pick(*refs):
        pick_kernel(heights, *refs)

    (coarse,) = call(pick, [coarse.shape], group_table, coarse, scalars=1)
    coarse = spread(coarse, "py")
    routed, start = [], 0
    for shape, height in zip(shapes, heights):
        routed.append(coarse[:, start : start + height, : shape[3]].reshape(shape))
        start += height
    return (modulus, routed[0], routed[1], routed[2])


def on_device(white_noise, spectrum, group_table):
    members, cells_x, cells_y, length_z = white_noise.shape
    size_px, size_py = lax.axis_size("px"), lax.axis_size("py")
    fits = members == 2 and length_z == 2 * LANES and 2 * cells_x * size_px == LANES
    fits = fits and cells_x * 2 == size_px * size_py
    fits = fits and size_px * size_px * size_py == LANES
    chosen = lanes_path if fits else general_path
    return chosen(white_noise, spectrum, group_table)


def solution(mesh):
    in_specs = (P(None, "px", "py", None), P("px", "py", None), P())
    out_specs = (P(None, "px", "py", None),) * 4
    return jax.shard_map(
        on_device, mesh=mesh, in_specs=in_specs, out_specs=out_specs, check_vma=False
    )
```

profile of v0, /device:TPU:0, one launch (start us, length us, event | category | flops | bytes accessed | tf_op | source)
XLA Modules:
  0.0 151.5 jit_solution(15421619341974383422)
XLA Ops:
  0.6 0.0 copy-start.5
  0.7 1.2 copy-done.5
  1.9 0.0 copy-start.6
  1.9 1.0 copy-done.6
  2.9 0.0 copy-start.8
  2.9 0.9 copy-done.8
  3.9 1.8 %shard_map.111.refs_0_ = f32[8,11,32,128]{3,2,1,0:T(8,128)S(1)} custom-call(f32[2,16,32,256]{3,2,1,0:T(8,128)S(1)} %copy-done.5, f32[16,32,256]{2,1,0:T(8,128)S(1)} %copy-done.6, f32[256,256]{1,0:T(8,128)S(1)} %copy-done.8), custom_call_target="tpu_custom_call" | custom-call | tf_op jit(solution)/shard_map/pallas_call | solution.py:419
  5.7 0.0 copy-start.3
  5.7 1.1 copy-done.3
  6.8 0.0 copy-start.4
  6.8 38.2 %shard_map.112.refs_0_ = f32[8,11,32,128]{3,2,1,0:T(8,128)} custom-call(f32[8,11,32,128]{3,2,1,0:T(8,128)} %copy-done.3), custom_call_target="tpu_custom_call" | custom-call | tf_op jit(solution)/shard_map/pallas_call | solution.py:391
  45.0 0.0 copy-done.4
  45.0 0.0 copy-start.2
  45.0 1.4 copy-done.2
  46.3 2.2 %shard_map.113.refs_0_ = f32[4,768,128]{2,1,0:T(8,128)S(1)} custom-call(f32[8,11,32,128]{3,2,1,0:T(8,128)S(1)} %copy-done.2, f32[512,256]{1,0:T(8,128)S(1)} %copy-done.4), custom_call_target="tpu_custom_call" | custom-call | tf_op jit(solution)/shard_map/pallas_call | solution.py:419
  48.5 0.0 copy-start.1
  48.5 1.2 copy-done.1
  49.7 0.0 copy-start.9
  49.7 0.0 copy-start.10
  49.7 15.7 %shard_map.114.refs_1_ = f32[4,768,128]{2,1,0:T(8,128)} custom-call(f32[4,768,128]{2,1,0:T(8,128)} %copy-done.1), custom_call_target="tpu_custom_call" | custom-call | tf_op jit(solution)/shard_map/pallas_call | solution.py:391
  65.4 0.0 copy-done.9
  65.4 0.0 copy-done.10
  65.4 0.0 copy-start
  65.4 1.4 copy-done
  66.8 2.8 %shard_map.115 = f32[4,512,128]{2,1,0:T(8,128)S(1)} custom-call(s32[1]{0:T(128)} %bitcast.refs_0_, f32[4,768,128]{2,1,0:T(8,128)S(1)} %copy-done, f32[128,128]{1,0:T(8,128)S(1)} %copy-done.10, f32[128,128]{1,0:T(8,128)S(1)} %copy-done.9), custom_call_target="tpu_custom_call" | custom-call | tf_op jit(solution)/shard_map/pallas_call | solution.py:419
  69.6 12.4 %all_to_all.20.refs_0_ = f32[4,512,128]{2,1,0:T(8,128)S(1)} all-to-all(f32[4,512,128]{2,1,0:T(8,128)S(1)} %shard_map.115), channel_id=1, replica_groups=mesh['px'=4,'py'=8] {'px'}, dimensions={0} | all-to-all | bytes 2097152 | tf_op jit(solution)/shard_map/all_to_all | solution.py:402
  82.0 2.2 %shard_map.116 = f32[8,8,32,128]{3,2,1,0:T(8,128)S(1)} custom-call(f32[4,512,128]{2,1,0:T(8,128)S(1)} %all_to_all.20.refs_0_, f32[512,256]{1,0:T(8,128)S(1)} %copy-done.4), custom_call_target="tpu_custom_call" | custom-call | tf_op jit(solution)/shard_map/pallas_call | solution.py:419
  84.1 0.0 copy-start.7
  84.1 0.0 copy-start.11
  84.2 37.5 %all_to_all.21.refs_0_ = f32[8,8,32,128]{3,2,1,0:T(8,128)S(1)} all-to-all(f32[8,8,32,128]{3,2,1,0:T(8,128)S(1)} %shard_map.116), channel_id=1, replica_groups=mesh['px'=4,'py'=8] {'py'}, dimensions={0} | all-to-all | bytes 2097152 | tf_op jit(solution)/shard_map/all_to_all | solution.py:402
  121.7 0.0 copy-done.7
  121.7 5.9 %shard_map.117 = (f32[2,16,32,256]{3,2,1,0:T(8,128)}, f32[8,42,128]{2,1,0:T(8,128)S(1)}) custom-call(f32[8,8,32,128]{3,2,1,0:T(8,128)S(1)} %all_to_all.21.refs_0_, f32[256,256]{1,0:T(8,128)S(1)} %copy-done.7), custom_call_target="tpu_custom_call" | custom-call | tf_op jit(solution)/shard_map/pallas_call | solution.py:419
  127.6 10.7 %all_to_all.22.refs_1_ = f32[8,42,128]{2,1,0:T(8,128)S(1)} all-to-all(f32[8,42,128]{2,1,0:T(8,128)S(1)} %get-tuple-element.7), channel_id=1, replica_groups=mesh['px'=4,'py'=8] {'py'}, dimensions={0} | all-to-all | bytes 344064 | tf_op jit(solution)/shard_map/all_to_all | solution.py:402
  138.3 0.0 copy-done.11
  138.3 0.6 shard_map.118
  138.9 10.7 %all_to_all.23 = f32[8,42,128]{2,1,0:T(8,128)S(1)} all-to-all(f32[8,42,128]{2,1,0:T(8,128)S(1)} %shard_map.118), channel_id=1, replica_groups=mesh['px'=4,'py'=8] {'py'}, dimensions={0} | all-to-all | bytes 344064 | tf_op jit(solution)/shard_map/all_to_all | solution.py:402
  149.6 0.6 slice.14
  150.2 0.6 slice.13
  150.9 0.7 slice.12
Async XLA Ops:
  0.6 1.2 copy-start.5
  1.9 1.0 copy-start.6
  2.9 0.9 copy-start.8
  5.7 1.1 copy-start.3
  6.8 38.2 %copy-start.4 = (f32[512,256]{1,0:T(8,128)S(1)}, f32[512,256]{1,0:T(8,128)}, u32[]{:S(2)}) copy-start(f32[512,256]{1,0:T(8,128)} %constant.24.clone.refs_1_) | copy-start | bytes 1572868
  45.0 1.4 copy-start.2
  48.5 1.2 copy-start.1
  49.7 15.7 %copy-start.9 = (f32[128,128]{1,0:T(8,128)S(1)}, f32[128,128]{1,0:T(8,128)}, u32[]{:S(2)}) copy-start(f32[128,128]{1,0:T(8,128)} %constant.26.clone.refs_3_) | copy-start | bytes 196612
  49.7 15.7 %copy-start.10 = (f32[128,128]{1,0:T(8,128)S(1)}, f32[128,128]{1,0:T(8,128)}, u32[]{:S(2)}) copy-start(f32[128,128]{1,0:T(8,128)} %constant.25.clone.refs_2_) | copy-start | bytes 196612
  65.4 1.4 copy-start
  84.1 37.6 %copy-start.7 = (f32[256,256]{1,0:T(8,128)S(1)}, f32[256,256]{1,0:T(8,128)}, u32[]{:S(2)}) copy-start(f32[256,256]{1,0:T(8,128)} %constant.30.refs_1_) | copy-start | bytes 786436
  84.1 54.2 %copy-start.11 = (s32[3,8]{1,0:T(4,128)S(1)}, s32[3,8]{1,0:T(4,128)}, u32[]{:S(2)}) copy-start(s32[3,8]{1,0:T(4,128)} %refs_0_.3) | copy-start | bytes 292
where the time goes:
time: 152 us
  blocking collectives  71.3 us (47%)
  Pallas kernels  69.3 us (46%)
  local copies, waits for them, and re-layouts  10.1 us (7%)
    all_to_all x4, blocking collectives, spread(): return lax.all_to_all(values, axis, split_axis=0, concat_axis=0, tiled=True)  71.3 us
    pallas_call x2, Pallas kernels, spread_call(): pl.pallas_call(body, out_shape=jax.ShapeDtypeStruct(values.shape, values....  53.9 us
    pallas_call x6, Pallas kernels, call(): pl.pallas_call(body, out_shape=out, in_specs=specs, out_specs=[pl.BlockSp...  15.4 us
    unnamed x24, local copies, waits for them, and re-layouts  8.27 us

commit v1 on v0

v1 whole, which is shorter than its diff:
```python
import numpy as np

import jax
import jax.numpy as jnp
from jax import lax
from jax.experimental import pallas as pl
from jax.experimental.pallas import tpu as pltpu
from jax.sharding import PartitionSpec as P


def angles_of(length):
    positions = np.arange(length, dtype=np.int64)
    return (positions[:, None] * positions[None, :] % length) * (2.0 * np.pi / length)


def complex_array(length, direction):
    angles = angles_of(length)
    cos, sin = np.cos(angles), direction * np.sin(angles)
    return np.stack([np.stack([cos, sin], 1), np.stack([-sin, cos], 1)], 0)


def complex_table(length, direction):
    return jnp.asarray(complex_array(length, direction), jnp.float32)


def half_tables(length):
    angles = angles_of(length)[:, : length // 2]
    ahead = np.stack([np.cos(angles), -np.sin(angles)], 1)
    back = 2.0 * ahead
    nyquist = np.where(np.arange(length) % 2 == 0, 1.0, -1.0)
    ahead[:, 1, 0] = nyquist
    back[:, 0, 0] = 1.0
    back[:, 1, 0] = nyquist
    return jnp.asarray(ahead, jnp.float32), jnp.asarray(back, jnp.float32)


def einsum(pattern, left, right):
    return jnp.einsum(pattern, left, right, precision=lax.Precision.HIGH)


def swap_first(values):
    first = values[:, :, :1]
    turned = jnp.swapaxes(first, 0, 1)
    return jnp.concatenate([turned, values[:, :, 1:]], 2)


def coarsen(values):
    members, size_x, size_y, size_z = values.shape
    blocks = values.reshape(members, size_x // 2, 2, size_y // 2, 2, size_z // 2, 2)
    return blocks.mean(axis=(2, 4, 6))


def general_path(white_noise, spectrum, group_table):
    members, cells_x, cells_y, length_z = white_noise.shape
    size_px, size_py = lax.axis_size("px"), lax.axis_size("py")
    length_x, length_y = cells_x * size_px, cells_y * size_py
    half_z = length_z // 2
    block_py, block = half_z // size_py, half_z // size_py // size_px
    z_ahead, z_back = half_tables(length_z)
    scale = 1.0 / (length_x * length_y * length_z)

    table = jnp.transpose(spectrum, (2, 0, 1))
    last = jnp.broadcast_to(table[half_z : half_z + 1], (size_py, 1, cells_x, cells_y))
    table = jnp.concatenate([table[:half_z].reshape(size_py, block_py, cells_x, cells_y), last], 1)
    table = lax.all_to_all(table, "py", split_axis=0, concat_axis=3, tiled=True)[0]
    last = jnp.broadcast_to(table[block_py:], (size_px, 1, cells_x, length_y))
    table = jnp.concatenate([table[:block_py].reshape(size_px, block, cells_x, length_y), last], 1)
    table = lax.all_to_all(table, "px", split_axis=0, concat_axis=2, tiled=True)[0] * scale
    is_first = (lax.axis_index("px") == 0) & (lax.axis_index("py") == 0)
    other = jnp.where(is_first, table[block:], table[:1])
    tables = jnp.stack([table[:block], jnp.concatenate([other, table[1:block]], 0)], 0)

    values = einsum("fxyz,zck->fckxy", white_noise, z_ahead)
    values = swap_first(values)
    values = lax.all_to_all(values, "py", split_axis=2, concat_axis=4, tiled=True)
    values = einsum("fckxy,cydm->fdkxm", values, complex_table(length_y, -1.0))
    values = lax.all_to_all(values, "px", split_axis=2, concat_axis=3, tiled=True)
    values = einsum("fckxm,cxdj->fdkjm", values, complex_table(length_x, -1.0))
    values = values * tables[:, None]
    values = einsum("fckjm,cjdx->fdkxm", values, complex_table(length_x, 1.0))
    values = lax.all_to_all(values, "px", split_axis=3, concat_axis=2, tiled=True)
    values = einsum("fckxm,cmdy->fdkxy", values, complex_table(length_y, 1.0))
    values = lax.all_to_all(values, "py", split_axis=4, concat_axis=2, tiled=True)
    values = swap_first(values)
    fields = einsum("fckxy,zck->fxyz", values, z_back)
    modulus = jnp.exp(0.5 * fields)

    levels = []
    level = modulus
    for _ in range(3):
        level = coarsen(level)
        levels.append(level)
    pieces = [jnp.reshape(level, (size_py, -1)) for level in levels]
    widths = [piece.shape[1] for piece in pieces]
    joined = jnp.concatenate(pieces, 1)
    spread = lax.all_to_all(joined, "py", split_axis=0, concat_axis=0, tiled=True)
    picked, start = [], 0
    for index, width in enumerate(widths):
        part = spread[:, start : start + width]
        picked.append(jnp.take(part, group_table[index], axis=0))
        start += width
    joined = lax.all_to_all(
        jnp.concatenate(picked, 1), "py", split_axis=0, concat_axis=0, tiled=True
    )
    routed, start = [], 0
    for level, width in zip(levels, widths):
        routed.append(joined[:, start : start + width].reshape(level.shape))
        start += width
    return (modulus, routed[0], routed[1], routed[2])


LANES = 128
MESH = pl.DeviceIdType.MESH
BF16 = jnp.bfloat16
F32 = jnp.float32


def halves(values):
    high = values.astype(BF16)
    low = (values - high.astype(F32)).astype(BF16)
    return high, low


def host_halves(values):
    values = np.asarray(values, np.float64)
    high = values.astype(np.float32).astype(BF16)
    low = (values - high.astype(np.float64)).astype(np.float32).astype(BF16)
    return jnp.asarray(high), jnp.asarray(low)


def mm(left, right):
    return jnp.dot(left, right, preferred_element_type=F32)


def lane_of(shape):
    return lax.broadcasted_iota(jnp.int32, shape, len(shape) - 1)


def exchange(arrays, width):
    arrays = list(arrays)
    lane = lane_of(arrays[0].shape)
    distance = 1
    while distance < len(arrays):
        step = distance * width
        low = (lane // step) % 2 == 0
        for index in range(len(arrays)):
            if (index // distance) % 2 == 0:
                first, second = arrays[index], arrays[index + distance]
                arrays[index] = jnp.where(low, first, pltpu.roll(second, step, 1))
                arrays[index + distance] = jnp.where(
                    low, pltpu.roll(first, LANES - step, 1), second
                )
        distance *= 2
    return arrays


def turned(values, slots, ahead):
    real = (lane_of(values.shape) // slots) % 2 == 0
    from_imag = pltpu.roll(values, LANES - slots, 1)
    from_real = pltpu.roll(values, slots, 1)
    if ahead:
        return jnp.where(real, from_imag, -from_real)
    return jnp.where(real, -from_imag, from_real)


def swap_slot(first, second, slots):
    place = lane_of(first.shape) % (2 * slots)
    return (
        jnp.where(place == slots, pltpu.roll(second, slots, 1), first),
        jnp.where(place == 0, pltpu.roll(first, LANES - slots, 1), second),
    )


class Route:
    def __init__(self, axis, count, away, source, target, send, recv):
        self.axis, self.count, self.away = axis, count, away
        self.source, self.target = source, target
        self.send, self.recv = send, recv
        self.me = lax.axis_index(axis)

    def copy(self, source, target, peer, part):
        return pltpu.make_async_remote_copy(
            src_ref=source,
            dst_ref=target,
            send_sem=self.send,
            recv_sem=self.recv.at[part] if part is not None else self.recv,
            device_id={self.axis: peer},
            device_id_type=MESH,
        )

    def at(self, ref, where, index):
        return ref.at[where + (index,)]

    def start(self, where, part):
        for peer in self.away:
            source = self.at(self.source, where, peer)
            target = self.at(self.target, where, self.me)
            self.copy(source, target, peer, part).start()

    def arrive(self, where, part):
        spot = self.at(self.target, where, pl.ds(0, self.count - 1))
        self.copy(spot, spot, self.away[0], part).wait_recv()
        self.target[where + (self.me,)] = self.source[where + (self.me,)]

    def drain(self, where):
        spot = self.source.at[where + (pl.ds(0, self.count - 1),)]
        self.copy(spot, spot, self.away[0], 0 if len(self.recv.shape) else None).wait_send()


def whole_kernel(sizes, loads, *refs):
    cells_x, cells_y, length_z, slots, ranks_y = sizes
    members = 2
    width = 2 * slots
    per_tile = cells_x // ranks_y
    tiles = length_z // LANES
    chunks = tiles * per_tile
    length_y = cells_y * ranks_y
    blocks = slots // members
    rows_m = length_y // blocks
    (group_table, *sources) = refs[: 1 + loads]
    modulus_out, level_one, level_two, level_three = refs[1 + loads : 5 + loads]
    held_in = refs[5 + loads : 5 + 2 * loads]
    (
        z_send, z_recv, x_send, x_recv, w_send, w_recv, b_send, b_recv,
        s_send, s_recv, t_send, t_recv, n_send, n_recv, m_recv,
        tables, other, held, modulus, c_send, c_recv_0, c_recv_1, d_send, d_recv,
        load_sem, store_sem, send_sem, z_sem, x_sem, w_sem, b_sem, c_sem, d_sem, s_sem,
    ) = refs[5 + 2 * loads :]
    (
        spectrum, noise, ahead_hi, ahead_lo, y_hi, y_lo, x_ahead, x_back,
        back_hi, back_lo, pool_rows, pool_columns,
    ) = held_in

    me_x, me_y = lax.axis_index("px"), lax.axis_index("py")
    copies = [
        pltpu.make_async_copy(source, target, load_sem.at[index])
        for index, (source, target) in enumerate(zip(sources, held_in))
    ]
    for copy in copies:
        copy.start()

    place, core = me_y // 2, me_y % 2
    chips = ranks_y // 2
    near = chips - 1 - (chips - 2) * (place % 2)
    steps = [chips // 2, near, chips - near]
    away_y = []
    for step in steps:
        for side in (0, 1):
            away_y.append((place + step) % chips * 2 + (core + side) % 2)
    away_y.append(place * 2 + 1 - core)
    away_x = [slots - 1 - me_x, (me_x + 2) % slots, me_x + 1 - 2 * (me_x % 2)]

    barrier = pltpu.get_barrier_semaphore()
    for peer in away_y:
        pl.semaphore_signal(barrier, inc=1, device_id={"py": peer}, device_id_type=MESH)
    for peer in away_x:
        pl.semaphore_signal(barrier, inc=1, device_id={"px": peer}, device_id_type=MESH)

    def route(axis, source, target, send, recv):
        away, count = (away_y, ranks_y) if axis == "py" else (away_x, slots)
        return Route(axis, count, away, source, target, send_sem.at[send], recv)

    z_route = route("py", z_send, z_recv, 0, z_sem)
    x_route = route("px", x_send, x_recv, 1, x_sem)
    w_route = route("px", w_send, w_recv, 2, w_sem)
    b_route = route("py", b_send, b_recv, 3, b_sem)
    s_route = route("py", s_send, s_recv, 4, s_sem.at[0])
    t_route = route("px", t_send, t_recv, 5, s_sem.at[1])
    c_recv = (c_recv_0, c_recv_1)
    c_routes = [route("py", c_send.at[f], c_recv[f], 6, c_sem.at[f]) for f in range(members)]
    d_route = route("py", d_send, d_recv, 7, d_sem)

    copies[0].wait()
    for row in range(0, cells_y, 8):
        rows = pl.ds(row, 8)
        moved = exchange([spectrum[x, rows, pl.ds(0, LANES)] for x in range(cells_x)], width)
        for group in range(cells_x):
            s_send[group % ranks_y, group // ranks_y, rows] = moved[group]
    lane = lane_of((8, LANES))
    strip = jnp.zeros((8, LANES), F32)
    quarter = (lane // 2) % slots
    for x in range(cells_x):
        for part in range(cells_y // 8):
            value = spectrum[x, pl.ds(part * 8, 8), pl.ds(LANES, 1)]
            strip = jnp.where((lane // width == x) & (quarter == part), value, strip)
    n_send[...] = strip

    pl.semaphore_wait(barrier, ranks_y + slots - 2)
    s_route.start((), None)

    def strip_copy():
        return pltpu.make_async_remote_copy(
            src_ref=n_send, dst_ref=n_recv.at[me_y], send_sem=send_sem.at[8],
            recv_sem=s_sem.at[2], device_id={"py": 0}, device_id_type=MESH,
        )

    pl.when(me_y != 0)(lambda: strip_copy().start())

    copies[1].wait()
    copies[2].wait()
    copies[3].wait()
    cells = cells_x * cells_y
    for f in range(members):
        high, low = halves(noise[f].reshape(cells, length_z))
        held[f] = mm(high, ahead_hi[...]) + mm(high, ahead_lo[...]) + mm(low, ahead_hi[...])
    for tile in range(tiles):
        lanes = pl.ds(tile * LANES, LANES)
        for row in range(0, cells_y, 8):
            rows = pl.ds(row, 8)
            both = []
            for f in range(members):
                both.append(
                    exchange(
                        [held[f, pl.ds(x * cells_y + row, 8), lanes] for x in range(cells_x)],
                        width,
                    )
                )
            if tile == 0:
                both[0][0], both[1][0] = swap_slot(both[0][0], both[1][0], slots)
            for f in range(members):
                for group in range(cells_x):
                    chunk = tile * per_tile + group // ranks_y
                    z_send[chunk, group % ranks_y, f, rows] = both[f][group]
        for part in range(per_tile):
            chunk = tile * per_tile + part
            z_route.start((chunk,), chunk)

    s_route.arrive((), None)
    for row in range(0, rows_m, 8):
        arrays = []
        for tile in range(tiles):
            for block in range(blocks):
                at = block * rows_m + row
                arrays.append(s_recv[at // cells_y, tile, pl.ds(at % cells_y, 8)])
        moved = exchange(arrays, 2)
        for rank in range(slots):
            t_send[rank, pl.ds(row, 8)] = moved[rank]
    t_route.start((), None)

    def strips_copy(source):
        return pltpu.make_async_remote_copy(
            src_ref=n_recv, dst_ref=m_recv.at[source], send_sem=send_sem.at[9],
            recv_sem=s_sem.at[3], device_id={"px": 0}, device_id_type=MESH,
        )

    @pl.when(me_y == 0)
    def _():
        spot = n_recv.at[pl.ds(0, ranks_y - 1)]
        pltpu.make_async_remote_copy(
            src_ref=spot, dst_ref=spot, send_sem=send_sem.at[8], recv_sem=s_sem.at[2],
            device_id={"py": 1}, device_id_type=MESH,
        ).wait_recv()
        n_recv[0] = n_send[...]
        pl.when(me_x != 0)(lambda: strips_copy(me_x).start())

    def along_y(route, part, columns, ahead):
        high, low = halves(columns)
        product = mm(y_hi[...], high) + mm(y_hi[...], low) + mm(y_lo[...], high)
        return product

    def combined(product, f, start, rows, ahead):
        lanes = slice(f * LANES, (f + 1) * LANES)
        by_cos = product[start : start + rows, lanes]
        by_sin = product[length_y + start : length_y + start + rows, lanes]
        return by_cos + turned(by_sin, slots, ahead)

    def y_ahead(chunk):
        z_route.arrive((chunk,), chunk)
        columns = [z_recv[chunk, :, f].reshape(length_y, LANES) for f in range(members)]
        product = along_y(z_route, chunk, jnp.concatenate(columns, 1), True)
        for row in range(0, rows_m, 16):
            arrays = []
            for f in range(members):
                for block in range(blocks):
                    arrays.append(combined(product, f, block * rows_m + row, 16, True))
            moved = exchange(arrays, 1)
            for rank in range(slots):
                x_send[chunk, rank, pl.ds(row, 16)] = moved[rank]
        x_route.start((chunk,), chunk)

    def gathered(ref, chunk):
        pieces = [[] for _ in range(slots)]
        for row in range(0, rows_m, 16):
            moved = exchange([ref[chunk, s, pl.ds(row, 16)] for s in range(slots)], 1)
            for index in range(slots):
                pieces[index].append(moved[index])
        return [jnp.concatenate(piece, 0) for piece in pieces]

    def along_x(values, table):
        product = mm(jnp.concatenate(halves(values), 1), table[...])
        return product[:, :LANES] + product[:, LANES:]

    def x_both(chunk):
        x_route.arrive((chunk,), chunk)
        values = along_x(jnp.concatenate(gathered(x_recv, chunk), 0), x_ahead)
        scaled = []
        for f in range(members):
            for block in range(blocks):
                at = (f * blocks + block) * rows_m
                table = other[block] if f == 1 and chunk == 0 else tables[chunk, block]
                scaled.append(values[at : at + rows_m] * table)
        values = along_x(jnp.concatenate(scaled, 0), x_back)
        for row in range(0, rows_m, 16):
            arrays = [values[a * rows_m + row : a * rows_m + row + 16] for a in range(slots)]
            moved = exchange(arrays, 1)
            for s in range(slots):
                w_send[chunk, s, pl.ds(row, 16)] = moved[s]
        w_route.start((chunk,), chunk)

    def y_back(chunk):
        w_route.arrive((chunk,), chunk)
        arrays = gathered(w_recv, chunk)
        columns = [
            jnp.concatenate(arrays[f * blocks : (f + 1) * blocks], 0) for f in range(members)
        ]
        product = along_y(w_route, chunk, jnp.concatenate(columns, 1), False)
        for f in range(members):
            for p in range(ranks_y):
                b_send[chunk, f, p] = combined(product, f, p * cells_y, cells_y, False)
            b_route.start((chunk, f), chunk * members + f)

    def spectrum_tables():
        t_route.arrive((), None)
        for row in range(0, rows_m, 8):
            rows = pl.ds(row, 8)
            moved = exchange([t_recv[s, rows] for s in range(slots)], 2)
            even = lane % 2 == 0
            for tile in range(tiles):
                for block in range(blocks):
                    part = moved[tile * blocks + block]
                    first = jnp.where(even, part, pltpu.roll(part, 1, 1))
                    second = jnp.where(even, pltpu.roll(part, LANES - 1, 1), part)
                    tables[tile * per_tile, block, rows] = first
                    tables[tile * per_tile + 1, block, rows] = second
                    if tile == 0:
                        other[block, rows] = first

        @pl.when((me_y == 0) & (me_x == 0))
        def _():
            spot = m_recv.at[pl.ds(1, slots - 1)]
            pltpu.make_async_remote_copy(
                src_ref=spot, dst_ref=spot, send_sem=send_sem.at[9], recv_sem=s_sem.at[3],
                device_id={"px": 1}, device_id_type=MESH,
            ).wait_recv()
            for p in range(ranks_y):
                strips = [n_recv[p] if s == 0 else m_recv[s, p] for s in range(slots)]
                for part in range(cells_y // 8):
                    value = strips[part]
                    for s in range(slots):
                        shift = (s - part) * 2 % LANES
                        moved = pltpu.roll(strips[s], shift, 1) if shift else strips[s]
                        value = jnp.where(quarter == s, moved, value)
                    at = p * cells_y + part * 8
                    other[at // rows_m, pl.ds(at % rows_m, 8)] = value

    for copy in copies[4:]:
        copy.wait()
    y_ahead(0)
    spectrum_tables()
    for step in range(1, chunks + 2):
        if step < chunks:
            y_ahead(step)
        if 0 <= step - 1 < chunks:
            x_both(step - 1)
        if 0 <= step - 2 < chunks:
            y_back(step - 2)

    low_rows = lax.broadcasted_iota(jnp.int32, (8, LANES), 0)
    tall = cells // 4 // ranks_y
    stores = []

    def z_back(f):
        arriving = [(chunk, f) for chunk in range(1, chunks)]
        for chunk, g in arriving + ([(0, g) for g in range(members)] if f == 0 else []):
            b_route.arrive((chunk, g), chunk * members + g)
        for tile in range(tiles):
            for row in range(0, cells_y, 8):
                rows = pl.ds(row, 8)
                arrays = []
                for group in range(cells_x):
                    chunk = tile * per_tile + group // ranks_y
                    arrays.append(b_recv[chunk, f, group % ranks_y, rows])
                if tile == 0:
                    pair = [b_recv[0, 0, 0, rows], b_recv[0, 1, 0, rows]]
                    arrays[0] = swap_slot(*pair, slots)[f]
                moved = exchange(arrays, width)
                for x in range(cells_x):
                    at = pl.ds(x * cells_y + row, 8)
                    held[f, at, pl.ds(tile * LANES, LANES)] = moved[x]
        high, low = halves(held[f])
        fields = mm(high, back_hi[...]) + mm(high, back_lo[...]) + mm(low, back_hi[...])
        values = jnp.exp(0.5 * fields)
        modulus[f] = values.reshape(cells_x, cells_y, length_z)
        store = pltpu.make_async_copy(modulus.at[f], modulus_out.at[f], store_sem.at[f])
        store.start()
        stores.append(store)
        high, low = halves(values)
        pooled = mm(pool_rows[...], high) + mm(pool_rows[...], low)
        high, low = halves(pooled)
        coarse = mm(high, pool_columns[...]) + mm(low, pool_columns[...])
        for d in range(ranks_y):
            at = ranks_y * tall + d * 8
            c_send[f, d, pl.ds(0, tall)] = coarse[d * tall : (d + 1) * tall, :LANES]
            c_send[f, d, pl.ds(tall, 8)] = coarse[at : at + 8, LANES:]
        c_routes[f].start((), None)

    def pick(f):
        c_routes[f].arrive((), None)
        for g in range(ranks_y):
            d_send[f, g, pl.ds(0, tall)] = c_recv[f][group_table[0, g], pl.ds(0, tall)]
            second = c_recv[f][group_table[1, g], pl.ds(tall, 8)]
            third = c_recv[f][group_table[2, g], pl.ds(tall, 8)]
            d_send[f, g, pl.ds(tall, 8)] = jnp.where(low_rows < 4, second, third)
        d_route.start((f,), f)

    def place_levels(f):
        d_route.arrive((f,), f)
        for d in range(ranks_y):
            level_one[f, d] = d_recv[f, d, pl.ds(0, tall)]
        lows = [d_recv[f, d, pl.ds(tall, 8)] for d in range(ranks_y)]
        half_y = cells_y // 4
        for x in range(ranks_y // 2):
            value = jnp.where(low_rows < 4, lows[2 * x], pltpu.roll(lows[2 * x + 1], 4, 0))
            level_two[f, x] = value[:half_y, : length_z // 4]
        for x in range(ranks_y // 4):
            value = lows[4 * x]
            for y in range(4):
                value = jnp.where(low_rows == y, pltpu.roll(lows[4 * x + y], (y + 4) % 8, 0), value)
            value = pltpu.roll(value, LANES // 2, 1)
            level_three[f, x] = value[: half_y // 2, : length_z // 8]

    z_back(0)
    z_back(1)
    pick(0)
    pick(1)
    place_levels(0)
    place_levels(1)

    every = pl.ds(0, chunks)
    z_route.drain((every,))
    x_route.drain((every,))
    w_route.drain((every,))
    b_route.drain((every, pl.ds(0, members)))
    s_route.drain(())
    t_route.drain(())
    spot = c_send.at[:, pl.ds(0, ranks_y - 1)]
    c_routes[0].copy(spot, spot, away_y[0], None).wait_send()
    d_route.drain((pl.ds(0, members),))
    pl.when(me_y != 0)(lambda: strip_copy().wait_send())
    pl.when((me_y == 0) & (me_x != 0))(lambda: strips_copy(me_x).wait_send())
    for store in stores:
        store.wait()


def lanes_path(white_noise, spectrum, group_table):
    members, cells_x, cells_y, length_z = white_noise.shape
    size_px, size_py = lax.axis_size("px"), lax.axis_size("py")
    length_x, length_y = cells_x * size_px, cells_y * size_py
    slots, width = size_px, 2 * size_px
    tiles = length_z // LANES
    per_tile = cells_x // size_py
    chunks = tiles * per_tile
    blocks = slots // members
    rows_m = length_y // blocks

    column = np.arange(length_z)
    tile, lane = column // LANES, column % LANES
    part = (lane // slots) % 2
    group = lane // width
    rank_q, rank_p, inner = lane % slots, group % size_py, group // size_py
    k = ((tile * size_py + rank_p) * slots + rank_q) * per_tile + inner
    angles = angles_of(length_z)
    sign = np.where(np.arange(length_z) % 2 == 0, 1.0, -1.0)
    z_ahead = np.where(part == 0, np.cos(angles[:, k]), -np.sin(angles[:, k]))
    z_back = 2.0 * z_ahead
    first = (k == 0) & (part == 0)
    second = (k == 0) & (part == 1)
    z_ahead[:, second] = sign[:, None]
    z_back[:, first] = 1.0
    z_back[:, second] = sign[:, None]
    z_back = z_back.T / (length_x * length_y * length_z)

    angles = angles_of(length_y)
    y_table = np.concatenate([np.cos(angles), np.sin(angles)], 0)

    lane = np.arange(LANES)
    cell = (lane // slots % 2, lane % slots * cells_x + lane // width)
    mode = (lane % 2, lane // 2 % slots * cells_x + lane // width)

    def x_table(direction, rows, columns):
        table = complex_array(length_x, direction)[rows][:, columns[0], columns[1]]
        high, low = host_halves(table)
        return jnp.concatenate(
            [
                jnp.concatenate([high, low], 1),
                jnp.concatenate([high, jnp.zeros_like(low)], 1),
            ],
            0,
        )

    def pool(extent_x, extent_y, factor):
        short_x, short_y = extent_x // factor, extent_y // factor
        row, cell = np.arange(short_x * short_y), np.arange(extent_x * extent_y)
        same_x = cell[None] // extent_y // factor == row[:, None] // short_y
        same_y = cell[None] % extent_y // factor == row[:, None] % short_y
        return np.where(same_x & same_y, 1.0 / factor**3, 0.0)

    second, third = pool(cells_x, cells_y, 4), pool(cells_x, cells_y, 8)
    lower = np.zeros((size_py, 8, cells_x * cells_y))
    lower[:, :4] = second.reshape(size_py, 4, -1)
    lower[:, 4:5] = third.reshape(size_py, 1, -1)
    pool_rows = np.concatenate([pool(cells_x, cells_y, 2), lower.reshape(8 * size_py, -1)], 0)
    pool_columns = np.zeros((length_z, 2 * LANES))
    z = np.arange(length_z)
    pool_columns[z, z // 2] = 1.0
    pool_columns[z, LANES + z // 4] = 1.0
    pool_columns[z, LANES + length_z // 4 + z // 8] = 1.0

    held_in = [
        spectrum,
        white_noise,
        *host_halves(z_ahead),
        *host_halves(y_table),
        x_table(-1.0, cell, mode),
        x_table(1.0, mode, cell),
        *host_halves(z_back),
        jnp.asarray(pool_rows, BF16),
        jnp.asarray(pool_columns, BF16),
    ]
    sizes = (cells_x, cells_y, length_z, slots, size_py)

    def body(*refs):
        whole_kernel(sizes, len(held_in), *refs)

    def vmem(*shape):
        return pltpu.VMEM(shape, F32)

    z_shape = (chunks, size_py, members, cells_y, LANES)
    x_shape = (chunks, slots, rows_m, LANES)
    b_shape = (chunks, members, size_py, cells_y, LANES)
    s_shape = (size_py, tiles, cells_y, LANES)
    t_shape = (slots, rows_m, LANES)
    height = cells_x * cells_y // 4 // size_py + 8
    c_shape = (members, size_py, height, LANES)
    sem = pltpu.SemaphoreType.DMA
    scratch = [pltpu.VMEM(value.shape, value.dtype) for value in held_in]
    for shape in (z_shape, x_shape, x_shape, b_shape, s_shape, t_shape):
        scratch += [vmem(*shape), vmem(*shape)]
    scratch += [vmem(8, LANES), vmem(size_py, 8, LANES), vmem(slots, size_py, 8, LANES)]
    scratch += [
        vmem(chunks, blocks, rows_m, LANES),
        vmem(blocks, rows_m, LANES),
        vmem(members, cells_x * cells_y, length_z),
        vmem(*white_noise.shape),
        vmem(*c_shape),
        vmem(*c_shape[1:]),
        vmem(*c_shape[1:]),
        vmem(*c_shape),
        vmem(*c_shape),
    ]
    scratch += [
        sem((len(held_in),)), sem((members,)), sem((10,)), sem((chunks,)), sem((chunks,)),
        sem((chunks,)), sem((chunks * members,)), sem((members,)), sem((members,)), sem((4,)),
    ]
    outs = [white_noise.shape]
    for level in range(1, 4):
        outs.append((members,) + tuple(extent >> level for extent in white_noise.shape[1:]))
    hbm = pl.BlockSpec(memory_space=pl.ANY)
    local = pl.BlockSpec(memory_space=pltpu.VMEM)
    return tuple(
        pl.pallas_call(
            body,
            out_shape=[jax.ShapeDtypeStruct(shape, F32) for shape in outs],
            in_specs=[pl.BlockSpec(memory_space=pltpu.SMEM)] + [hbm] * len(held_in),
            out_specs=[hbm, local, local, local],
            scratch_shapes=scratch,
            compiler_params=pltpu.CompilerParams(
                collective_id=0, has_side_effects=True, vmem_limit_bytes=56 * 1024 * 1024
            ),
        )(group_table, *held_in)
    )


def on_device(white_noise, spectrum, group_table):
    members, cells_x, cells_y, length_z = white_noise.shape
    size_px, size_py = lax.axis_size("px"), lax.axis_size("py")
    fits = members == 2 and length_z == 2 * LANES and size_px == 4 and size_py == 8
    fits = fits and 2 * cells_x * size_px == LANES and cells_x == 2 * size_py
    fits = fits and cells_y == 2 * cells_x
    chosen = lanes_path if fits else general_path
    return chosen(white_noise, spectrum, group_table)


def solution(mesh):
    in_specs = (P(None, "px", "py", None), P("px", "py", None), P())
    out_specs = (P(None, "px", "py", None),) * 4
    return jax.shard_map(
        on_device, mesh=mesh, in_specs=in_specs, out_specs=out_specs, check_vma=False
    )
```

time: 152 us -> 81.6 us (0.54)
  blocking collectives: 71.3 us -> 0 us
  Pallas kernels: 69.3 us -> 76.3 us
  local copies, waits for them, and re-layouts: 10.1 us -> 4.41 us
    all_to_all x4 -> x0, blocking collectives: 71.3 us -> none  [spread(): return lax.all_to_all(values, axis, split_axis=0, concat_axis=0, tiled=True)]
    pallas_call x8 -> x1, Pallas kernels: 69.3 us -> 76.3 us  [lanes_path(): pl.pallas_call(body, out_shape=[jax.ShapeDtypeStruct(shape, F32) for shap...]
    unnamed x24 -> x10, local copies, waits for them, and re-layouts: 8.27 us -> 4.41 us
    slice x3 -> x0, local copies, waits for them, and re-layouts: 1.88 us -> none  [lanes_path(): routed.append(coarse[:, start:start + height, :shape[3]].reshape(shape))]
where the time goes in v1:
time: 81.6 us; the launch traced here: 81.3 us
  Pallas kernels  76.3 us (94%)
  local copies, waits for them, and re-layouts  4.41 us (5%)
    pallas_call x1, Pallas kernels, lanes_path(): pl.pallas_call(body, out_shape=[jax.ShapeDtypeStruct(shape, F32) for shap...  76.3 us
    unnamed x10, local copies, waits for them, and re-layouts  4.41 us

profile of v1, /device:TPU:0, one launch (start us, length us, event | category | flops | bytes accessed | tf_op | source)
XLA Modules:
  0.0 81.3 jit_solution(10823798429559658794)
XLA Ops:
  0.6 76.3 %shard_map.174 = (f32[2,16,32,256]{3,2,1,0:T(8,128)}, f32[2,8,16,128]{3,2,1,0:T(8,128)}, f32[2,4,8,64]{3,2,1,0:T(8,128)}, f32[2,2,4,32]{3,2,1,0:T(4,128)}) custom-call(s32[3,8]{1,0:T(4,128)} %refs_0_.1, f32[16,32,256]{2,1,0:T(8,128)} %refs_1_.1, f32[2,16,32,256]{3,2,1,0:T(8,128)} %refs_2_.1, bf16[256,256]{1,0:T(8,128)(2,1)} %constant.26.clone.refs_3_, ...), custom_call_target="tpu_custom_call" | custom-call | tf_op jit(solution)/shard_map/pallas_call | solution.py:671
  76.9 0.0 copy-start
  76.9 2.3 %copy.23 = f32[2,16,32,256]{3,2,1,0:T(8,128)} copy(f32[2,16,32,256]{3,2,1,0:T(8,128)} %get-tuple-element.8) | data formatting | bytes 2097152
  79.3 0.0 copy-done
  79.3 0.0 copy-start.1
  79.3 0.7 copy.24
  79.9 0.1 copy-done.1
  80.0 0.0 copy-start.2
  80.0 0.6 copy.25
  80.6 0.1 copy-done.2
  80.7 0.6 copy.26
Async XLA Ops:
  76.9 2.4 %copy-start = (f32[2,8,16,128]{3,2,1,0:T(8,128)S(1)}, f32[2,8,16,128]{3,2,1,0:T(8,128)}, u32[]{:S(2)}) copy-start(f32[2,8,16,128]{3,2,1,0:T(8,128)} %get-tuple-element.9) | copy-start | bytes 393220
  79.3 0.8 copy-start.1
  80.0 0.7 copy-start.2

commit v2 on v1

--- a/solution.py
+++ b/solution.py
@@ -110,6 +110,7 @@
 
 
 LANES = 128
+PARTS = 2
 MESH = pl.DeviceIdType.MESH
 BF16 = jnp.bfloat16
 F32 = jnp.float32
@@ -217,18 +218,19 @@
     length_y = cells_y * ranks_y
     blocks = slots // members
     rows_m = length_y // blocks
-    (group_table, *sources) = refs[: 1 + loads]
-    modulus_out, level_one, level_two, level_three = refs[1 + loads : 5 + loads]
-    held_in = refs[5 + loads : 5 + 2 * loads]
+    parts = PARTS
+    rows_part = rows_m // parts
+    sources, held_in = refs[:loads], refs[2 + loads : 2 + 2 * loads]
+    modulus, d_recv = refs[loads : 2 + loads]
     (
         z_send, z_recv, x_send, x_recv, w_send, w_recv, b_send, b_recv,
-        s_send, s_recv, t_send, t_recv, n_send, n_recv, m_recv,
-        tables, other, held, modulus, c_send, c_recv_0, c_recv_1, d_send, d_recv,
-        load_sem, store_sem, send_sem, z_sem, x_sem, w_sem, b_sem, c_sem, d_sem, s_sem,
-    ) = refs[5 + 2 * loads :]
+        s_send, s_recv, e_recv, t_send, t_recv, n_send, n_recv, m_recv,
+        tables, other, held, h_recv, c_send, c_recv_0, c_recv_1, d_send,
+        load_sem, send_sem, z_sem, x_sem, w_sem, b_sem, c_sem, d_sem, s_sem, h_sem,
+    ) = refs[2 + 2 * loads :]
     (
-        spectrum, noise, ahead_hi, ahead_lo, y_hi, y_lo, x_ahead, x_back,
-        back_hi, back_lo, pool_rows, pool_columns,
+        spectrum, mirror_z, noise, ahead_hi, ahead_lo, mirror_x, mirror_y, y_hi, y_lo, x_ahead, x_back,
+        back_hi, back_lo, pool_rows, pool_columns, group_table,
     ) = held_in
 
     me_x, me_y = lax.axis_index("px"), lax.axis_index("py")
@@ -264,19 +266,31 @@
     x_route = route("px", x_send, x_recv, 1, x_sem)
     w_route = route("px", w_send, w_recv, 2, w_sem)
     b_route = route("py", b_send, b_recv, 3, b_sem)
-    s_route = route("py", s_send, s_recv, 4, s_sem.at[0])
     t_route = route("px", t_send, t_recv, 5, s_sem.at[1])
     c_recv = (c_recv_0, c_recv_1)
     c_routes = [route("py", c_send.at[f], c_recv[f], 6, c_sem.at[f]) for f in range(members)]
     d_route = route("py", d_send, d_recv, 7, d_sem)
 
+    lane = lane_of((8, LANES))
+    half_y = ranks_y // 2
+    my_half, my_place = me_y // half_y, me_y % half_y
     copies[0].wait()
+    copies[1].wait()
+    mirrored = jnp.concatenate(
+        halves(spectrum[:, :, LANES : 2 * LANES].reshape(cells_x * cells_y, LANES)), 1
+    )
+    held[0, :, pl.ds(0, LANES)] = mm(mirrored, mirror_z[...])
     for row in range(0, cells_y, 8):
         rows = pl.ds(row, 8)
-        moved = exchange([spectrum[x, rows, pl.ds(0, LANES)] for x in range(cells_x)], width)
-        for group in range(cells_x):
-            s_send[group % ranks_y, group // ranks_y, rows] = moved[group]
-    lane = lane_of((8, LANES))
+        plain = [spectrum[x, rows, pl.ds(0, LANES)] for x in range(cells_x)]
+        turned_z = []
+        for x in range(cells_x):
+            value = held[0, pl.ds(x * cells_y + row, 8), pl.ds(0, LANES)]
+            turned_z.append(jnp.where(lane == 0, plain[x], value))
+        for kind, arrays in enumerate((plain, turned_z)):
+            moved = exchange(arrays, width)
+            for group in range(cells_x):
+                s_send[group % ranks_y, kind, group // ranks_y, rows] = moved[group]
     strip = jnp.zeros((8, LANES), F32)
     quarter = (lane // 2) % slots
     for x in range(cells_x):
@@ -285,20 +299,72 @@
             strip = jnp.where((lane // width == x) & (quarter == part), value, strip)
     n_send[...] = strip
 
-    pl.semaphore_wait(barrier, ranks_y + slots - 2)
-    s_route.start((), None)
-
     def strip_copy():
         return pltpu.make_async_remote_copy(
             src_ref=n_send, dst_ref=n_recv.at[me_y], send_sem=send_sem.at[8],
             recv_sem=s_sem.at[2], device_id={"py": 0}, device_id_type=MESH,
         )
 
-    pl.when(me_y != 0)(lambda: strip_copy().start())
-
-    copies[1].wait()
-    copies[2].wait()
-    copies[3].wait()
+    def half_copy(peer):
+        return pltpu.make_async_remote_copy(
+            src_ref=s_send.at[peer], dst_ref=s_recv.at[my_place], send_sem=send_sem.at[4],
+            recv_sem=s_sem.at[0], device_id={"py": peer}, device_id_type=MESH,
+        )
+
+    def edge_copy(peer):
+        return pltpu.make_async_remote_copy(
+            src_ref=s_send.at[peer, 1, :, pl.ds(0, 8)], dst_ref=e_recv, send_sem=send_sem.at[10],
+            recv_sem=s_sem.at[4], device_id={"py": peer}, device_id_type=MESH,
+        )
+
+    others = [my_half * half_y + (my_place + step) % half_y for step in range(1, half_y)]
+    across = [(1 - my_half) * half_y + step for step in range(half_y)]
+
+    def send_spectrum():
+        pl.when(me_y != 0)(lambda: strip_copy().start())
+        for peer in others[1:] + others[:1]:
+            half_copy(peer).start()
+
+        @pl.when(my_place == 0)
+        def _():
+            for peer in across:
+                edge_copy(peer).start()
+
+    middle = (place == chips // 2) | (place == chips // 2 - 1)
+    giver, taker = middle & (core == 0), middle & (core == 1)
+
+    def hand_copy(chunk):
+        return pltpu.make_async_remote_copy(
+            src_ref=z_send.at[chunk, pl.ds((1 - my_half) * half_y, half_y)],
+            dst_ref=h_recv.at[chunk], send_sem=send_sem.at[0], recv_sem=h_sem.at[chunk],
+            device_id={"py": place * 2 + 1 - core}, device_id_type=MESH,
+        )
+
+    def z_copy(source, chunk, slot, peer, send):
+        return pltpu.make_async_remote_copy(
+            src_ref=source, dst_ref=z_recv.at[chunk, slot], send_sem=send_sem.at[send],
+            recv_sem=z_sem.at[chunk], device_id={"py": peer}, device_id_type=MESH,
+        )
+
+    def z_start(chunk):
+        @pl.when(giver)
+        def _():
+            hand_copy(chunk).start()
+            for peer in others:
+                z_copy(z_send.at[chunk, peer], chunk, me_y, peer, 0).start()
+
+        @pl.when(jnp.logical_not(giver))
+        def _():
+            z_route.start((chunk,), chunk)
+
+        @pl.when(taker)
+        def _():
+            hand_copy(chunk).wait_recv()
+            for step, peer in enumerate(across):
+                z_copy(h_recv.at[chunk, step], chunk, me_y - 1, peer, 11).start()
+
+    for copy in copies[2:6]:
+        copy.wait()
     cells = cells_x * cells_y
     for f in range(members):
         high, low = halves(noise[f].reshape(cells, length_z))
@@ -321,17 +387,34 @@
                 for group in range(cells_x):
                     chunk = tile * per_tile + group // ranks_y
                     z_send[chunk, group % ranks_y, f, rows] = both[f][group]
+        if tile == 0:
+            pl.semaphore_wait(barrier, ranks_y + slots - 2)
+            send_spectrum()
         for part in range(per_tile):
             chunk = tile * per_tile + part
-            z_route.start((chunk,), chunk)
-
-    s_route.arrive((), None)
+            z_start(chunk)
+
+    spot = s_recv.at[pl.ds(0, half_y - 1)]
+    pltpu.make_async_remote_copy(
+        src_ref=spot, dst_ref=spot, send_sem=send_sem.at[4], recv_sem=s_sem.at[0],
+        device_id={"py": others[0]}, device_id_type=MESH,
+    ).wait_recv()
+    edge_copy(others[0]).wait_recv()
+    s_recv[my_place] = s_send[me_y]
+    copies[6].wait()
+    copies[7].wait()
+    pair = [s_recv[:, 1, tile].reshape(rows_m, LANES) for tile in range(tiles)]
+    pair = jnp.concatenate(halves(jnp.concatenate(pair, 1)), 0)
+    held[1, pl.ds(0, rows_m)] = mm(mirror_y[...], pair)
+    sublane = lax.broadcasted_iota(jnp.int32, (8, LANES), 0)
     for row in range(0, rows_m, 8):
         arrays = []
         for tile in range(tiles):
-            for block in range(blocks):
-                at = block * rows_m + row
-                arrays.append(s_recv[at // cells_y, tile, pl.ds(at % cells_y, 8)])
+            arrays.append(s_recv[row // cells_y, 0, tile, pl.ds(row % cells_y, 8)])
+            value = held[1, pl.ds(row, 8), pl.ds(tile * LANES, LANES)]
+            if row == 0:
+                value = jnp.where(sublane == 0, e_recv[tile], value)
+            arrays.append(value)
         moved = exchange(arrays, 2)
         for rank in range(slots):
             t_send[rank, pl.ds(row, 8)] = moved[rank]
@@ -343,16 +426,6 @@
             recv_sem=s_sem.at[3], device_id={"px": 0}, device_id_type=MESH,
         )
 
-    @pl.when(me_y == 0)
-    def _():
-        spot = n_recv.at[pl.ds(0, ranks_y - 1)]
-        pltpu.make_async_remote_copy(
-            src_ref=spot, dst_ref=spot, send_sem=send_sem.at[8], recv_sem=s_sem.at[2],
-            device_id={"py": 1}, device_id_type=MESH,
-        ).wait_recv()
-        n_recv[0] = n_send[...]
-        pl.when(me_x != 0)(lambda: strips_copy(me_x).start())
-
     def along_y(route, part, columns, ahead):
         high, low = halves(columns)
         product = mm(y_hi[...], high) + mm(y_hi[...], low) + mm(y_lo[...], high)
@@ -368,22 +441,25 @@
         z_route.arrive((chunk,), chunk)
         columns = [z_recv[chunk, :, f].reshape(length_y, LANES) for f in range(members)]
         product = along_y(z_route, chunk, jnp.concatenate(columns, 1), True)
-        for row in range(0, rows_m, 16):
-            arrays = []
-            for f in range(members):
-                for block in range(blocks):
-                    arrays.append(combined(product, f, block * rows_m + row, 16, True))
-            moved = exchange(arrays, 1)
-            for rank in range(slots):
-                x_send[chunk, rank, pl.ds(row, 16)] = moved[rank]
-        x_route.start((chunk,), chunk)
-
-    def gathered(ref, chunk):
+        for part in range(parts):
+            for row in range(0, rows_part, 16):
+                arrays = []
+                for f in range(members):
+                    for block in range(blocks):
+                        at = block * rows_m + part * rows_part + row
+                        arrays.append(combined(product, f, at, 16, True))
+                moved = exchange(arrays, 1)
+                for rank in range(slots):
+                    x_send[chunk, part, rank, pl.ds(row, 16)] = moved[rank]
+            x_route.start((chunk, part), chunk * parts + part)
+
+    def gathered(ref, chunk, some):
         pieces = [[] for _ in range(slots)]
-        for row in range(0, rows_m, 16):
-            moved = exchange([ref[chunk, s, pl.ds(row, 16)] for s in range(slots)], 1)
-            for index in range(slots):
-                pieces[index].append(moved[index])
+        for part in some:
+            for row in range(0, rows_part, 16):
+                moved = exchange([ref[chunk, part, s, pl.ds(row, 16)] for s in range(slots)], 1)
+                for index in range(slots):
+                    pieces[index].append(moved[index])
         return [jnp.concatenate(piece, 0) for piece in pieces]
 
     def along_x(values, table):
@@ -391,25 +467,30 @@
         return product[:, :LANES] + product[:, LANES:]
 
     def x_both(chunk):
-        x_route.arrive((chunk,), chunk)
-        values = along_x(jnp.concatenate(gathered(x_recv, chunk), 0), x_ahead)
-        scaled = []
-        for f in range(members):
-            for block in range(blocks):
-                at = (f * blocks + block) * rows_m
-                table = other[block] if f == 1 and chunk == 0 else tables[chunk, block]
-                scaled.append(values[at : at + rows_m] * table)
-        values = along_x(jnp.concatenate(scaled, 0), x_back)
-        for row in range(0, rows_m, 16):
-            arrays = [values[a * rows_m + row : a * rows_m + row + 16] for a in range(slots)]
-            moved = exchange(arrays, 1)
-            for s in range(slots):
-                w_send[chunk, s, pl.ds(row, 16)] = moved[s]
-        w_route.start((chunk,), chunk)
+        for part in range(parts):
+            x_route.arrive((chunk, part), chunk * parts + part)
+            values = along_x(jnp.concatenate(gathered(x_recv, chunk, [part]), 0), x_ahead)
+            scaled = []
+            rows = pl.ds(part * rows_part, rows_part)
+            for f in range(members):
+                for block in range(blocks):
+                    at = (f * blocks + block) * rows_part
+                    table = other if f == 1 and chunk == 0 else tables.at[chunk]
+                    scaled.append(values[at : at + rows_part] * table[block, rows])
+            values = along_x(jnp.concatenate(scaled, 0), x_back)
+            for row in range(0, rows_part, 16):
+                arrays = [
+                    values[a * rows_part + row : a * rows_part + row + 16] for a in range(slots)
+                ]
+                moved = exchange(arrays, 1)
+                for s in range(slots):
+                    w_send[chunk, part, s, pl.ds(row, 16)] = moved[s]
+            w_route.start((chunk, part), chunk * parts + part)
 
     def y_back(chunk):
-        w_route.arrive((chunk,), chunk)
-        arrays = gathered(w_recv, chunk)
+        for part in range(parts):
+            w_route.arrive((chunk, part), chunk * parts + part)
+        arrays = gathered(w_recv, chunk, range(parts))
         columns = [
             jnp.concatenate(arrays[f * blocks : (f + 1) * blocks], 0) for f in range(members)
         ]
@@ -419,21 +500,30 @@
                 b_send[chunk, f, p] = combined(product, f, p * cells_y, cells_y, False)
             b_route.start((chunk, f), chunk * members + f)
 
+    def table_rows(tile, block, rows, part):
+        even = lane % 2 == 0
+        first = jnp.where(even, part, pltpu.roll(part, 1, 1))
+        second = jnp.where(even, pltpu.roll(part, LANES - 1, 1), part)
+        tables[tile * per_tile, block, rows] = first
+        tables[tile * per_tile + 1, block, rows] = second
+        if tile == 0:
+            other[block, rows] = first
+
     def spectrum_tables():
         t_route.arrive((), None)
+        images = [[] for _ in range(tiles)]
         for row in range(0, rows_m, 8):
             rows = pl.ds(row, 8)
             moved = exchange([t_recv[s, rows] for s in range(slots)], 2)
-            even = lane % 2 == 0
             for tile in range(tiles):
-                for block in range(blocks):
-                    part = moved[tile * blocks + block]
-                    first = jnp.where(even, part, pltpu.roll(part, 1, 1))
-                    second = jnp.where(even, pltpu.roll(part, LANES - 1, 1), part)
-                    tables[tile * per_tile, block, rows] = first
-                    tables[tile * per_tile + 1, block, rows] = second
-                    if tile == 0:
-                        other[block, rows] = first
+                table_rows(tile, my_half, rows, moved[2 * tile])
+                images[tile].append(moved[2 * tile + 1])
+        images = jnp.concatenate([piece for pieces in images for piece in pieces], 0)
+        images = mm(jnp.concatenate(halves(images), 1), mirror_x[...])
+        for tile in range(tiles):
+            for row in range(0, rows_m, 8):
+                at = tile * rows_m + row
+                table_rows(tile, 1 - my_half, pl.ds(row, 8), images[at : at + 8])
 
         @pl.when((me_y == 0) & (me_x == 0))
         def _():
@@ -453,21 +543,28 @@
                     at = p * cells_y + part * 8
                     other[at // rows_m, pl.ds(at % rows_m, 8)] = value
 
-    for copy in copies[4:]:
+    @pl.when(me_y == 0)
+    def _():
+        spot = n_recv.at[pl.ds(0, ranks_y - 1)]
+        pltpu.make_async_remote_copy(
+            src_ref=spot, dst_ref=spot, send_sem=send_sem.at[8], recv_sem=s_sem.at[2],
+            device_id={"py": 1}, device_id_type=MESH,
+        ).wait_recv()
+        n_recv[0] = n_send[...]
+        pl.when(me_x != 0)(lambda: strips_copy(me_x).start())
+
+    for copy in copies[8:]:
         copy.wait()
     y_ahead(0)
     spectrum_tables()
-    for step in range(1, chunks + 2):
-        if step < chunks:
-            y_ahead(step)
-        if 0 <= step - 1 < chunks:
-            x_both(step - 1)
-        if 0 <= step - 2 < chunks:
-            y_back(step - 2)
+    for chunk in range(chunks):
+        x_both(chunk)
+        if chunk + 1 < chunks:
+            y_ahead(chunk + 1)
+        y_back(chunk)
 
     low_rows = lax.broadcasted_iota(jnp.int32, (8, LANES), 0)
     tall = cells // 4 // ranks_y
-    stores = []
 
     def z_back(f):
         arriving = [(chunk, f) for chunk in range(1, chunks)]
@@ -491,9 +588,6 @@
         fields = mm(high, back_hi[...]) + mm(high, back_lo[...]) + mm(low, back_hi[...])
         values = jnp.exp(0.5 * fields)
         modulus[f] = values.reshape(cells_x, cells_y, length_z)
-        store = pltpu.make_async_copy(modulus.at[f], modulus_out.at[f], store_sem.at[f])
-        store.start()
-        stores.append(store)
         high, low = halves(values)
         pooled = mm(pool_rows[...], high) + mm(pool_rows[...], low)
         high, low = halves(pooled)
@@ -513,43 +607,74 @@
             d_send[f, g, pl.ds(tall, 8)] = jnp.where(low_rows < 4, second, third)
         d_route.start((f,), f)
 
-    def place_levels(f):
-        d_route.arrive((f,), f)
-        for d in range(ranks_y):
-            level_one[f, d] = d_recv[f, d, pl.ds(0, tall)]
-        lows = [d_recv[f, d, pl.ds(tall, 8)] for d in range(ranks_y)]
-        half_y = cells_y // 4
-        for x in range(ranks_y // 2):
-            value = jnp.where(low_rows < 4, lows[2 * x], pltpu.roll(lows[2 * x + 1], 4, 0))
-            level_two[f, x] = value[:half_y, : length_z // 4]
-        for x in range(ranks_y // 4):
-            value = lows[4 * x]
-            for y in range(4):
-                value = jnp.where(low_rows == y, pltpu.roll(lows[4 * x + y], (y + 4) % 8, 0), value)
-            value = pltpu.roll(value, LANES // 2, 1)
-            level_three[f, x] = value[: half_y // 2, : length_z // 8]
-
     z_back(0)
     z_back(1)
     pick(0)
     pick(1)
-    place_levels(0)
-    place_levels(1)
+    d_route.arrive((0,), 0)
+    d_route.arrive((1,), 1)
 
     every = pl.ds(0, chunks)
     z_route.drain((every,))
-    x_route.drain((every,))
-    w_route.drain((every,))
+
+    @pl.when(taker)
+    def _():
+        pltpu.make_async_remote_copy(
+            src_ref=h_recv, dst_ref=h_recv, send_sem=send_sem.at[11], recv_sem=h_sem.at[0],
+            device_id={"py": others[0]}, device_id_type=MESH,
+        ).wait_send()
+
+    x_route.drain((every, pl.ds(0, parts)))
+    w_route.drain((every, pl.ds(0, parts)))
     b_route.drain((every, pl.ds(0, members)))
-    s_route.drain(())
+    spot = s_send.at[pl.ds(0, half_y - 1)]
+    pltpu.make_async_remote_copy(
+        src_ref=spot, dst_ref=spot, send_sem=send_sem.at[4], recv_sem=s_sem.at[0],
+        device_id={"py": others[0]}, device_id_type=MESH,
+    ).wait_send()
+
+    @pl.when(my_place == 0)
+    def _():
+        spot = s_send.at[pl.ds(0, half_y), 1, :, pl.ds(0, 8)]
+        pltpu.make_async_remote_copy(
+            src_ref=spot, dst_ref=spot, send_sem=send_sem.at[10], recv_sem=s_sem.at[4],
+            device_id={"py": others[0]}, device_id_type=MESH,
+        ).wait_send()
+
     t_route.drain(())
     spot = c_send.at[:, pl.ds(0, ranks_y - 1)]
     c_routes[0].copy(spot, spot, away_y[0], None).wait_send()
     d_route.drain((pl.ds(0, members),))
     pl.when(me_y != 0)(lambda: strip_copy().wait_send())
     pl.when((me_y == 0) & (me_x != 0))(lambda: strips_copy(me_x).wait_send())
-    for store in stores:
-        store.wait()
+
+
+def leaving_kernel(modulus, coarse, modulus_out, one_out, level_two, level_three, sems):
+    members, cells_x, cells_y, length_z = modulus.shape
+    ranks_y, tall = coarse.shape[1], coarse.shape[2] - 8
+    copies = [
+        pltpu.make_async_copy(modulus.at[f], modulus_out.at[f], sems.at[f]) for f in range(members)
+    ]
+    copies.append(
+        pltpu.make_async_copy(coarse.at[:, :, pl.ds(0, tall)], one_out, sems.at[members])
+    )
+    for copy in copies:
+        copy.start()
+    low_rows = lax.broadcasted_iota(jnp.int32, (8, LANES), 0)
+    short = cells_y // 4
+    for f in range(members):
+        lows = [coarse[f, d, pl.ds(tall, 8)] for d in range(ranks_y)]
+        for x in range(ranks_y // 2):
+            value = jnp.where(low_rows < 4, lows[2 * x], pltpu.roll(lows[2 * x + 1], 4, 0))
+            level_two[f, x] = value[:short, : length_z // 4]
+        for x in range(ranks_y // 4):
+            value = lows[4 * x]
+            for y in range(4):
+                value = jnp.where(low_rows == y, pltpu.roll(lows[4 * x + y], (y + 4) % 8, 0), value)
+            value = pltpu.roll(value, LANES // 2, 1)
+            level_three[f, x] = value[: short // 2, : length_z // 8]
+    for copy in copies:
+        copy.wait()
 
 
 def lanes_path(white_noise, spectrum, group_table):
@@ -598,6 +723,15 @@
             0,
         )
 
+    at = np.arange(1, LANES)
+    mirror_z = np.zeros((LANES, LANES))
+    mirror_z[LANES - at, at] = 1.0
+    at = np.arange(1, rows_m)
+    mirror_y = np.zeros((rows_m, rows_m))
+    mirror_y[at, rows_m - at] = 1.0
+    same = (mode[1][:, None] + mode[1][None]) % length_x == 0
+    mirror_x = np.where(same & (mode[0][:, None] == mode[0][None]), 1.0, 0.0)
+
     def pool(extent_x, extent_y, factor):
         short_x, short_y = extent_x // factor, extent_y // factor
         row, cell = np.arange(short_x * short_y), np.arange(extent_x * extent_y)
@@ -618,14 +752,18 @@
 
     held_in = [
         spectrum,
+        jnp.asarray(np.tile(mirror_z, (2, 1)), BF16),
         white_noise,
         *host_halves(z_ahead),
+        jnp.asarray(np.tile(mirror_x, (2, 1)), BF16),
+        jnp.asarray(np.tile(mirror_y, (1, 2)), BF16),
         *host_halves(y_table),
         x_table(-1.0, cell, mode),
         x_table(1.0, mode, cell),
         *host_halves(z_back),
         jnp.asarray(pool_rows, BF16),
         jnp.asarray(pool_columns, BF16),
+        group_table,
     ]
     sizes = (cells_x, cells_y, length_z, slots, size_py)
 
@@ -636,48 +774,58 @@
         return pltpu.VMEM(shape, F32)
 
     z_shape = (chunks, size_py, members, cells_y, LANES)
-    x_shape = (chunks, slots, rows_m, LANES)
+    x_shape = (chunks, PARTS, slots, rows_m // PARTS, LANES)
     b_shape = (chunks, members, size_py, cells_y, LANES)
-    s_shape = (size_py, tiles, cells_y, LANES)
+    s_shape = (2, tiles, cells_y, LANES)
     t_shape = (slots, rows_m, LANES)
     height = cells_x * cells_y // 4 // size_py + 8
     c_shape = (members, size_py, height, LANES)
     sem = pltpu.SemaphoreType.DMA
-    scratch = [pltpu.VMEM(value.shape, value.dtype) for value in held_in]
-    for shape in (z_shape, x_shape, x_shape, b_shape, s_shape, t_shape):
+    scratch = [pltpu.VMEM(value.shape, value.dtype) for value in held_in[:-1]]
+    scratch.append(pltpu.SMEM(group_table.shape, group_table.dtype))
+    for shape in (z_shape, x_shape, x_shape, b_shape):
         scratch += [vmem(*shape), vmem(*shape)]
+    scratch += [vmem(size_py, *s_shape), vmem(size_py // 2, *s_shape), vmem(tiles, 8, LANES)]
+    scratch += [vmem(*t_shape), vmem(*t_shape)]
     scratch += [vmem(8, LANES), vmem(size_py, 8, LANES), vmem(slots, size_py, 8, LANES)]
     scratch += [
         vmem(chunks, blocks, rows_m, LANES),
         vmem(blocks, rows_m, LANES),
         vmem(members, cells_x * cells_y, length_z),
-        vmem(*white_noise.shape),
+        vmem(chunks, size_py // 2, members, cells_y, LANES),
         vmem(*c_shape),
         vmem(*c_shape[1:]),
         vmem(*c_shape[1:]),
         vmem(*c_shape),
-        vmem(*c_shape),
     ]
     scratch += [
-        sem((len(held_in),)), sem((members,)), sem((10,)), sem((chunks,)), sem((chunks,)),
-        sem((chunks,)), sem((chunks * members,)), sem((members,)), sem((members,)), sem((4,)),
+        sem((len(held_in),)), sem((12,)), sem((chunks,)), sem((chunks * PARTS,)),
+        sem((chunks * PARTS,)), sem((chunks * members,)), sem((members,)), sem((members,)), sem((5,)), sem((chunks,)),
     ]
+    hbm = pl.BlockSpec(memory_space=pltpu.HBM)
+    local = pl.BlockSpec(memory_space=pltpu.VMEM)
+    modulus, coarse = pl.pallas_call(
+        body,
+        out_shape=[jax.ShapeDtypeStruct(shape, F32) for shape in (white_noise.shape, c_shape)],
+        in_specs=[hbm] * len(held_in),
+        out_specs=[local, local],
+        scratch_shapes=scratch,
+        compiler_params=pltpu.CompilerParams(
+            collective_id=0, has_side_effects=True, vmem_limit_bytes=40 * 1024 * 1024
+        ),
+    )(*[pltpu.with_memory_space_constraint(v, pltpu.HBM) for v in held_in])
     outs = [white_noise.shape]
     for level in range(1, 4):
         outs.append((members,) + tuple(extent >> level for extent in white_noise.shape[1:]))
-    hbm = pl.BlockSpec(memory_space=pl.ANY)
-    local = pl.BlockSpec(memory_space=pltpu.VMEM)
     return tuple(
         pl.pallas_call(
-            body,
+            leaving_kernel,
             out_shape=[jax.ShapeDtypeStruct(shape, F32) for shape in outs],
-            in_specs=[pl.BlockSpec(memory_space=pltpu.SMEM)] + [hbm] * len(held_in),
-            out_specs=[hbm, local, local, local],
-            scratch_shapes=scratch,
-            compiler_params=pltpu.CompilerParams(
-                collective_id=0, has_side_effects=True, vmem_limit_bytes=56 * 1024 * 1024
-            ),
-        )(group_table, *held_in)
+            in_specs=[local, local],
+            out_specs=[hbm, hbm, local, local],
+            scratch_shapes=[sem((members + 1,))],
+            compiler_params=pltpu.CompilerParams(vmem_limit_bytes=4 * 1024 * 1024),
+        )(modulus, coarse)
     )
 
 

time: 81.6 us -> 69.4 us (0.85)
  Pallas kernels: 76.3 us -> 68.4 us
  local copies, waits for them, and re-layouts: 4.41 us -> 0 us
    pallas_call x1, Pallas kernels: 76.3 us -> 66.8 us  [lanes_path(): pl.pallas_call(body, out_shape=[jax.ShapeDtypeStruct(shape, F32) for shap...]
    unnamed x10 -> x0, local copies, waits for them, and re-layouts: 4.41 us -> none
    pallas_call x0 -> x1, Pallas kernels: none -> 1.65 us  [lanes_path(): pl.pallas_call(leaving_kernel, out_shape=[jax.ShapeDtypeStruct(shape, F32...]
where the time goes in v2:
time: 69.4 us; the launch traced here: 69.2 us
  Pallas kernels  68.4 us (99%)
  between operations  0.8 us (1%)
    pallas_call x1, Pallas kernels, lanes_path(): pl.pallas_call(body, out_shape=[jax.ShapeDtypeStruct(shape, F32) for shap...  66.8 us
    pallas_call x1, Pallas kernels, lanes_path(): pl.pallas_call(leaving_kernel, out_shape=[jax.ShapeDtypeStruct(shape, F32...  1.65 us

profile of v2, /device:TPU:0, one launch (start us, length us, event | category | flops | bytes accessed | tf_op | source)
XLA Modules:
  0.0 69.2 jit_solution(1593803926260131401)
XLA Ops:
  0.6 66.8 %shard_map.201 = (f32[2,16,32,256]{3,2,1,0:T(8,128)S(1)}, f32[2,8,24,128]{3,2,1,0:T(8,128)S(1)}) custom-call(f32[16,32,256]{2,1,0:T(8,128)} %refs_0_.1, bf16[256,128]{1,0:T(8,128)(2,1)} %constant.32.clone.refs_1_, f32[2,16,32,256]{3,2,1,0:T(8,128)} %refs_2_.1, bf16[256,256]{1,0:T(8,128)(2,1)} %constant.33.clone.refs_3_, ...), custom_call_target="tpu_custom_call" | custom-call | tf_op jit(solution)/shard_map/pallas_call | solution.py:807
  67.4 1.6 %shard_map.202 = (f32[2,16,32,256]{3,2,1,0:T(8,128)}, f32[2,8,16,128]{3,2,1,0:T(8,128)}, f32[2,4,8,64]{3,2,1,0:T(8,128)}, f32[2,2,4,32]{3,2,1,0:T(4,128)}) custom-call(f32[2,16,32,256]{3,2,1,0:T(8,128)S(1)} %get-tuple-element.6.modulus, f32[2,8,24,128]{3,2,1,0:T(8,128)S(1)} %get-tuple-element.7.coarse), custom_call_target="tpu_custom_call" | custom-call | tf_op jit(solution)/shard_map/pallas_call | solution.py:821

commit v3 on v2

--- a/solution.py
+++ b/solution.py
@@ -138,21 +138,19 @@
 
 
 def exchange(arrays, width):
-    arrays = list(arrays)
-    lane = lane_of(arrays[0].shape)
+    count = len(arrays)
+    field = (lane_of(arrays[0].shape) // width) % count
+    skewed = [pltpu.roll(a, i * width, 1) if i else a for i, a in enumerate(arrays)]
+    moved = [skewed[-index % count] for index in range(count)]
     distance = 1
-    while distance < len(arrays):
-        step = distance * width
-        low = (lane // step) % 2 == 0
-        for index in range(len(arrays)):
-            if (index // distance) % 2 == 0:
-                first, second = arrays[index], arrays[index + distance]
-                arrays[index] = jnp.where(low, first, pltpu.roll(second, step, 1))
-                arrays[index + distance] = jnp.where(
-                    low, pltpu.roll(first, LANES - step, 1), second
-                )
+    while distance < count:
+        take = (field // distance) % 2 == 1
+        moved = [
+            jnp.where(take, moved[(index - distance) % count], moved[index])
+            for index in range(count)
+        ]
         distance *= 2
-    return arrays
+    return [pltpu.roll(m, LANES - i * width, 1) if i else m for i, m in enumerate(moved)]
 
 
 def turned(values, slots, ahead):
@@ -220,17 +218,18 @@
     rows_m = length_y // blocks
     parts = PARTS
     rows_part = rows_m // parts
-    sources, held_in = refs[:loads], refs[2 + loads : 2 + 2 * loads]
-    modulus, d_recv = refs[loads : 2 + loads]
+    sources, held_in = refs[:loads], refs[3 + loads : 3 + 2 * loads]
+    modulus, d_recv_0, d_recv_1 = refs[loads : 3 + loads]
     (
         z_send, z_recv, x_send, x_recv, w_send, w_recv, b_send, b_recv,
         s_send, s_recv, e_recv, t_send, t_recv, n_send, n_recv, m_recv,
-        tables, other, held, h_recv, c_send, c_recv_0, c_recv_1, d_send,
+        tables, other, held, partial, back_hi, back_lo, lower, h_recv, c_send_0, c_send_1, c_recv_0, c_recv_1,
+        d_send_0, d_send_1,
         load_sem, send_sem, z_sem, x_sem, w_sem, b_sem, c_sem, d_sem, s_sem, h_sem,
-    ) = refs[2 + 2 * loads :]
+    ) = refs[3 + 2 * loads :]
     (
         spectrum, mirror_z, noise, ahead_hi, ahead_lo, mirror_x, mirror_y, y_hi, y_lo, x_ahead, x_back,
-        back_hi, back_lo, pool_rows, pool_columns, group_table,
+        side_hi, side_lo, pool_rows, pool_columns, group_table,
     ) = held_in
 
     me_x, me_y = lax.axis_index("px"), lax.axis_index("py")
@@ -238,9 +237,6 @@
         pltpu.make_async_copy(source, target, load_sem.at[index])
         for index, (source, target) in enumerate(zip(sources, held_in))
     ]
-    for copy in copies:
-        copy.start()
-
     place, core = me_y // 2, me_y % 2
     chips = ranks_y // 2
     near = chips - 1 - (chips - 2) * (place % 2)
@@ -258,6 +254,10 @@
     for peer in away_x:
         pl.semaphore_signal(barrier, inc=1, device_id={"px": peer}, device_id_type=MESH)
 
+    early = 6
+    for copy in copies[:early]:
+        copy.start()
+
     def route(axis, source, target, send, recv):
         away, count = (away_y, ranks_y) if axis == "py" else (away_x, slots)
         return Route(axis, count, away, source, target, send_sem.at[send], recv)
@@ -267,9 +267,10 @@
     w_route = route("px", w_send, w_recv, 2, w_sem)
     b_route = route("py", b_send, b_recv, 3, b_sem)
     t_route = route("px", t_send, t_recv, 5, s_sem.at[1])
-    c_recv = (c_recv_0, c_recv_1)
-    c_routes = [route("py", c_send.at[f], c_recv[f], 6, c_sem.at[f]) for f in range(members)]
-    d_route = route("py", d_send, d_recv, 7, d_sem)
+    c_send, c_recv = (c_send_0, c_send_1), (c_recv_0, c_recv_1)
+    d_send, d_recv = (d_send_0, d_send_1), (d_recv_0, d_recv_1)
+    c_routes = [route("py", c_send[f], c_recv[f], 12 + f, c_sem.at[f]) for f in range(members)]
+    d_routes = [route("py", d_send[f], d_recv[f], 14 + f, d_sem.at[f]) for f in range(members)]
 
     lane = lane_of((8, LANES))
     half_y = ranks_y // 2
@@ -363,8 +364,10 @@
             for step, peer in enumerate(across):
                 z_copy(h_recv.at[chunk, step], chunk, me_y - 1, peer, 11).start()
 
-    for copy in copies[2:6]:
+    for copy in copies[2:early]:
         copy.wait()
+    for copy in copies[early:]:
+        copy.start()
     cells = cells_x * cells_y
     for f in range(members):
         high, low = halves(noise[f].reshape(cells, length_z))
@@ -394,6 +397,19 @@
             chunk = tile * per_tile + part
             z_start(chunk)
 
+    for copy in copies[early:]:
+        copy.wait()
+    sides = cells_x // ranks_y
+    rows_side = LANES // sides
+    for target, source, count in ((back_hi, side_hi, 2), (back_lo, side_lo, 1)):
+        blank = jnp.zeros((rows_side, length_z), BF16)
+        for chunk in range(chunks):
+            for block in range(count * sides):
+                rows = pl.ds(block * rows_side, rows_side)
+                for side in range(sides):
+                    value = source[chunk] if block % sides == side else blank
+                    target[chunk, rows, pl.ds(side * length_z, length_z)] = value
+
     spot = s_recv.at[pl.ds(0, half_y - 1)]
     pltpu.make_async_remote_copy(
         src_ref=spot, dst_ref=spot, send_sem=send_sem.at[4], recv_sem=s_sem.at[0],
@@ -401,8 +417,6 @@
     ).wait_recv()
     edge_copy(others[0]).wait_recv()
     s_recv[my_place] = s_send[me_y]
-    copies[6].wait()
-    copies[7].wait()
     pair = [s_recv[:, 1, tile].reshape(rows_m, LANES) for tile in range(tiles)]
     pair = jnp.concatenate(halves(jnp.concatenate(pair, 1)), 0)
     held[1, pl.ds(0, rows_m)] = mm(mirror_y[...], pair)
@@ -553,8 +567,6 @@
         n_recv[0] = n_send[...]
         pl.when(me_x != 0)(lambda: strips_copy(me_x).start())
 
-    for copy in copies[8:]:
-        copy.wait()
     y_ahead(0)
     spectrum_tables()
     for chunk in range(chunks):
@@ -563,56 +575,74 @@
             y_ahead(chunk + 1)
         y_back(chunk)
 
-    low_rows = lax.broadcasted_iota(jnp.int32, (8, LANES), 0)
     tall = cells // 4 // ranks_y
-
-    def z_back(f):
-        arriving = [(chunk, f) for chunk in range(1, chunks)]
-        for chunk, g in arriving + ([(0, g) for g in range(members)] if f == 0 else []):
-            b_route.arrive((chunk, g), chunk * members + g)
-        for tile in range(tiles):
-            for row in range(0, cells_y, 8):
-                rows = pl.ds(row, 8)
-                arrays = []
-                for group in range(cells_x):
-                    chunk = tile * per_tile + group // ranks_y
-                    arrays.append(b_recv[chunk, f, group % ranks_y, rows])
-                if tile == 0:
-                    pair = [b_recv[0, 0, 0, rows], b_recv[0, 1, 0, rows]]
-                    arrays[0] = swap_slot(*pair, slots)[f]
-                moved = exchange(arrays, width)
-                for x in range(cells_x):
-                    at = pl.ds(x * cells_y + row, 8)
-                    held[f, at, pl.ds(tile * LANES, LANES)] = moved[x]
-        high, low = halves(held[f])
-        fields = mm(high, back_hi[...]) + mm(high, back_lo[...]) + mm(low, back_hi[...])
+    def z_back(chunk, f):
+        pieces = [[] for _ in range(ranks_y)]
+        for row in range(0, cells_y, 8):
+            rows = pl.ds(row, 8)
+            arrays = [b_recv[chunk, f, group, rows] for group in range(ranks_y)]
+            if chunk == 0:
+                pair = [b_recv[0, 0, 0, rows], b_recv[0, 1, 0, rows]]
+                arrays[0] = swap_slot(*pair, slots)[f]
+            moved = exchange(arrays, width)
+            for x in range(ranks_y):
+                pieces[x].append(moved[x])
+        high, low = halves(jnp.concatenate([piece for some in pieces for piece in some], 0))
+        fields = mm(jnp.concatenate([high, low], 1), back_hi[chunk]) + mm(high, back_lo[chunk])
+        if chunk > 0:
+            fields = fields + partial[f]
+        if chunk + 1 < chunks:
+            partial[f] = fields
+            return
         values = jnp.exp(0.5 * fields)
-        modulus[f] = values.reshape(cells_x, cells_y, length_z)
+        for side in range(sides):
+            lanes = slice(side * length_z, (side + 1) * length_z)
+            cut = values[:, lanes].reshape(ranks_y, cells_y, length_z)
+            modulus[f, pl.ds(side * ranks_y, ranks_y)] = cut
         high, low = halves(values)
         pooled = mm(pool_rows[...], high) + mm(pool_rows[...], low)
-        high, low = halves(pooled)
+        pooled = [pooled[:, side * length_z : (side + 1) * length_z] for side in range(sides)]
+        high, low = halves(jnp.concatenate(pooled, 0))
         coarse = mm(high, pool_columns[...]) + mm(low, pool_columns[...])
+        per_side = ranks_y // sides
+        height = coarse.shape[0] // sides
         for d in range(ranks_y):
-            at = ranks_y * tall + d * 8
-            c_send[f, d, pl.ds(0, tall)] = coarse[d * tall : (d + 1) * tall, :LANES]
-            c_send[f, d, pl.ds(tall, 8)] = coarse[at : at + 8, LANES:]
+            base = d // per_side * height
+            at = base + d % per_side * tall
+            c_send[f][d, pl.ds(0, tall)] = coarse[at : at + tall, :LANES]
+            at = base + per_side * tall + d % per_side * 8
+            value = coarse[at : at + 8, LANES:]
+            value = jnp.where(lane < LANES // 2, value, pltpu.roll(value, 4, 0))
+            if f == 0:
+                lower[d] = value
+            else:
+                c_send[f][d, pl.ds(tall, 8)] = jnp.where(
+                    sublane < 4, lower[d], pltpu.roll(value, 4, 0)
+                )
         c_routes[f].start((), None)
 
     def pick(f):
         c_routes[f].arrive((), None)
         for g in range(ranks_y):
-            d_send[f, g, pl.ds(0, tall)] = c_recv[f][group_table[0, g], pl.ds(0, tall)]
-            second = c_recv[f][group_table[1, g], pl.ds(tall, 8)]
-            third = c_recv[f][group_table[2, g], pl.ds(tall, 8)]
-            d_send[f, g, pl.ds(tall, 8)] = jnp.where(low_rows < 4, second, third)
-        d_route.start((f,), f)
-
-    z_back(0)
-    z_back(1)
-    pick(0)
-    pick(1)
-    d_route.arrive((0,), 0)
-    d_route.arrive((1,), 1)
+            d_send[f][g, pl.ds(0, tall)] = c_recv[f][group_table[0, g], pl.ds(0, tall)]
+            if f == 1:
+                second = c_recv[f][group_table[1, g], pl.ds(tall, 8)]
+                third = c_recv[f][group_table[2, g], pl.ds(tall, 8)]
+                d_send[f][g, pl.ds(tall, 8)] = jnp.where(lane < LANES // 2, second, third)
+        d_routes[f].start((), None)
+
+    for chunk in range(chunks):
+        for f in range(members):
+            b_route.arrive((chunk, f), chunk * members + f)
+            if chunk > 0:
+                z_back(chunk, f)
+        if chunk == 0:
+            for f in range(members):
+                z_back(chunk, f)
+    for f in range(members):
+        pick(f)
+    for f in range(members):
+        d_routes[f].arrive((), None)
 
     every = pl.ds(0, chunks)
     z_route.drain((every,))
@@ -642,35 +672,44 @@
         ).wait_send()
 
     t_route.drain(())
-    spot = c_send.at[:, pl.ds(0, ranks_y - 1)]
-    c_routes[0].copy(spot, spot, away_y[0], None).wait_send()
-    d_route.drain((pl.ds(0, members),))
+    for some in c_routes + d_routes:
+        some.drain(())
     pl.when(me_y != 0)(lambda: strip_copy().wait_send())
     pl.when((me_y == 0) & (me_x != 0))(lambda: strips_copy(me_x).wait_send())
 
 
-def leaving_kernel(modulus, coarse, modulus_out, one_out, level_two, level_three, sems):
+def leaving_kernel(modulus, first, second, modulus_out, one_out, level_two, level_three, sems):
     members, cells_x, cells_y, length_z = modulus.shape
-    ranks_y, tall = coarse.shape[1], coarse.shape[2] - 8
-    copies = [
-        pltpu.make_async_copy(modulus.at[f], modulus_out.at[f], sems.at[f]) for f in range(members)
-    ]
-    copies.append(
-        pltpu.make_async_copy(coarse.at[:, :, pl.ds(0, tall)], one_out, sems.at[members])
-    )
+    ranks_y, tall = first.shape[:2]
+    copies = []
+    for f, coarse in enumerate((first, second)):
+        copies.append(pltpu.make_async_copy(modulus.at[f], modulus_out.at[f], sems.at[f]))
+        copies.append(
+            pltpu.make_async_copy(
+                coarse.at[:, pl.ds(0, tall)], one_out.at[f], sems.at[members + f]
+            )
+        )
     for copy in copies:
         copy.start()
-    low_rows = lax.broadcasted_iota(jnp.int32, (8, LANES), 0)
+    row = lax.broadcasted_iota(jnp.int32, (8, LANES), 0)
     short = cells_y // 4
+    lows = [second[d, pl.ds(tall, 8)] for d in range(ranks_y)]
     for f in range(members):
-        lows = [coarse[f, d, pl.ds(tall, 8)] for d in range(ranks_y)]
+        shifts = [4 * f, 4 - 4 * f]
         for x in range(ranks_y // 2):
-            value = jnp.where(low_rows < 4, lows[2 * x], pltpu.roll(lows[2 * x + 1], 4, 0))
+            pair = [
+                pltpu.roll(low, shift, 0) if shift else low
+                for low, shift in zip(lows[2 * x : 2 * x + 2], shifts)
+            ]
+            value = jnp.where(row < 4, *pair)
             level_two[f, x] = value[:short, : length_z // 4]
         for x in range(ranks_y // 4):
-            value = lows[4 * x]
+            value = jnp.zeros((8, LANES), F32)
             for y in range(4):
-                value = jnp.where(low_rows == y, pltpu.roll(lows[4 * x + y], (y + 4) % 8, 0), value)
+                low = lows[4 * x + y]
+                shift = (y - 4 * f) % 8
+                low = pltpu.roll(low, shift, 0) if shift else low
+                value = jnp.where(row == y, low, value)
             value = pltpu.roll(value, LANES // 2, 1)
             level_three[f, x] = value[: short // 2, : length_z // 8]
     for copy in copies:
@@ -705,6 +744,10 @@
     z_back[:, second] = sign[:, None]
     z_back = z_back.T / (length_x * length_y * length_z)
 
+    sides = cells_x // size_py
+    half_cells = cells_x * cells_y // sides
+    back_hi, back_lo = host_halves(z_back.reshape(chunks, LANES // sides, length_z))
+
     angles = angles_of(length_y)
     y_table = np.concatenate([np.cos(angles), np.sin(angles)], 0)
 
@@ -739,11 +782,12 @@
         same_y = cell[None] % extent_y // factor == row[:, None] % short_y
         return np.where(same_x & same_y, 1.0 / factor**3, 0.0)
 
-    second, third = pool(cells_x, cells_y, 4), pool(cells_x, cells_y, 8)
-    lower = np.zeros((size_py, 8, cells_x * cells_y))
-    lower[:, :4] = second.reshape(size_py, 4, -1)
-    lower[:, 4:5] = third.reshape(size_py, 1, -1)
-    pool_rows = np.concatenate([pool(cells_x, cells_y, 2), lower.reshape(8 * size_py, -1)], 0)
+    per_side = size_py // sides
+    some = size_py, cells_y
+    lower = np.zeros((per_side, 8, half_cells))
+    lower[:, :4] = pool(*some, 4).reshape(per_side, 4, -1)
+    lower[:, 4:5] = pool(*some, 8).reshape(per_side, 1, -1)
+    pool_rows = np.concatenate([pool(*some, 2), lower.reshape(8 * per_side, -1)], 0)
     pool_columns = np.zeros((length_z, 2 * LANES))
     z = np.arange(length_z)
     pool_columns[z, z // 2] = 1.0
@@ -760,7 +804,8 @@
         *host_halves(y_table),
         x_table(-1.0, cell, mode),
         x_table(1.0, mode, cell),
-        *host_halves(z_back),
+        back_hi,
+        back_lo,
         jnp.asarray(pool_rows, BF16),
         jnp.asarray(pool_columns, BF16),
         group_table,
@@ -778,8 +823,8 @@
     b_shape = (chunks, members, size_py, cells_y, LANES)
     s_shape = (2, tiles, cells_y, LANES)
     t_shape = (slots, rows_m, LANES)
-    height = cells_x * cells_y // 4 // size_py + 8
-    c_shape = (members, size_py, height, LANES)
+    tall = cells_x * cells_y // 4 // size_py
+    c_shapes = [(size_py, tall, LANES), (size_py, tall + 8, LANES)]
     sem = pltpu.SemaphoreType.DMA
     scratch = [pltpu.VMEM(value.shape, value.dtype) for value in held_in[:-1]]
     scratch.append(pltpu.SMEM(group_table.shape, group_table.dtype))
@@ -792,23 +837,24 @@
         vmem(chunks, blocks, rows_m, LANES),
         vmem(blocks, rows_m, LANES),
         vmem(members, cells_x * cells_y, length_z),
+        vmem(members, half_cells, sides * length_z),
+        pltpu.VMEM((chunks, 2 * LANES, sides * length_z), BF16),
+        pltpu.VMEM((chunks, LANES, sides * length_z), BF16),
+        vmem(size_py, 8, LANES),
         vmem(chunks, size_py // 2, members, cells_y, LANES),
-        vmem(*c_shape),
-        vmem(*c_shape[1:]),
-        vmem(*c_shape[1:]),
-        vmem(*c_shape),
+        *[vmem(*shape) for shape in c_shapes * 3],
     ]
     scratch += [
-        sem((len(held_in),)), sem((12,)), sem((chunks,)), sem((chunks * PARTS,)),
+        sem((len(held_in),)), sem((16,)), sem((chunks,)), sem((chunks * PARTS,)),
         sem((chunks * PARTS,)), sem((chunks * members,)), sem((members,)), sem((members,)), sem((5,)), sem((chunks,)),
     ]
     hbm = pl.BlockSpec(memory_space=pltpu.HBM)
     local = pl.BlockSpec(memory_space=pltpu.VMEM)
-    modulus, coarse = pl.pallas_call(
+    leaving = pl.pallas_call(
         body,
-        out_shape=[jax.ShapeDtypeStruct(shape, F32) for shape in (white_noise.shape, c_shape)],
+        out_shape=[jax.ShapeDtypeStruct(shape, F32) for shape in [white_noise.shape] + c_shapes],
         in_specs=[hbm] * len(held_in),
-        out_specs=[local, local],
+        out_specs=[local] * 3,
         scratch_shapes=scratch,
         compiler_params=pltpu.CompilerParams(
             collective_id=0, has_side_effects=True, vmem_limit_bytes=40 * 1024 * 1024
@@ -821,11 +867,11 @@
         pl.pallas_call(
             leaving_kernel,
             out_shape=[jax.ShapeDtypeStruct(shape, F32) for shape in outs],
-            in_specs=[local, local],
+            in_specs=[local] * 3,
             out_specs=[hbm, hbm, local, local],
-            scratch_shapes=[sem((members + 1,))],
+            scratch_shapes=[sem((2 * members,))],
             compiler_params=pltpu.CompilerParams(vmem_limit_bytes=4 * 1024 * 1024),
-        )(modulus, coarse)
+        )(*leaving)
     )
 
 

time: 69.4 us -> 66.2 us (0.954)
  Pallas kernels: 68.4 us -> 65.2 us
    pallas_call x1, Pallas kernels: 66.8 us -> 63.6 us  [lanes_path(): pl.pallas_call(body, out_shape=[jax.ShapeDtypeStruct(shape, F32) for shap...]
where the time goes in v3:
time: 66.2 us; the launch traced here: 66 us
  Pallas kernels  65.2 us (98%)
  between operations  0.8 us (1%)
    pallas_call x1, Pallas kernels, lanes_path(): pl.pallas_call(body, out_shape=[jax.ShapeDtypeStruct(shape, F32) for shap...  63.6 us
    pallas_call x1, Pallas kernels, lanes_path(): pl.pallas_call(leaving_kernel, out_shape=[jax.ShapeDtypeStruct(shape, F32...  1.65 us

profile of v3, /device:TPU:0, one launch (start us, length us, event | category | flops | bytes accessed | tf_op | source)
XLA Modules:
  0.0 66.0 jit_solution(3784390692189090895)
XLA Ops:
  0.6 63.6 %shard_map.201 = (f32[2,16,32,256]{3,2,1,0:T(8,128)S(1)}, f32[8,16,128]{2,1,0:T(8,128)S(1)}, f32[8,24,128]{2,1,0:T(8,128)S(1)}) custom-call(f32[16,32,256]{2,1,0:T(8,128)} %refs_0_.1, bf16[256,128]{1,0:T(8,128)(2,1)} %constant.34.clone.refs_1_, f32[2,16,32,256]{3,2,1,0:T(8,128)} %refs_2_.1, bf16[256,256]{1,0:T(8,128)(2,1)} %constant.35.clone.refs_3_, ...), custom_call_target="tpu_custom_call" | custom-call | tf_op jit(solution)/shard_map/pallas_call | solution.py:853
  64.2 1.7 %shard_map.202 = (f32[2,16,32,256]{3,2,1,0:T(8,128)}, f32[2,8,16,128]{3,2,1,0:T(8,128)}, f32[2,4,8,64]{3,2,1,0:T(8,128)}, f32[2,2,4,32]{3,2,1,0:T(4,128)}) custom-call(f32[2,16,32,256]{3,2,1,0:T(8,128)S(1)} %get-tuple-element.7.modulus, f32[8,16,128]{2,1,0:T(8,128)S(1)} %get-tuple-element.8.first, f32[8,24,128]{2,1,0:T(8,128)S(1)} %get-tuple-element.9.second), custom_call_target="tpu_custom_call" | custom-call | tf_op jit(solution)/shard_map/pallas_call | solution.py:867

commit v4 on v3

--- a/solution.py
+++ b/solution.py
@@ -110,7 +110,10 @@
 
 
 LANES = 128
-PARTS = 2
+ORDER = (
+    "y0", "y1", "T", "y2", "x0", "y3", "x1", "y4", "x2", "b0", "x3", "y5", "b1",
+    "y6", "x4", "b2", "y7", "b3", "x5", "x6", "b4", "x7", "b5", "b6", "b7",
+)
 MESH = pl.DeviceIdType.MESH
 BF16 = jnp.bfloat16
 F32 = jnp.float32
@@ -216,19 +219,18 @@
     length_y = cells_y * ranks_y
     blocks = slots // members
     rows_m = length_y // blocks
-    parts = PARTS
-    rows_part = rows_m // parts
+    rows_part = length_y // slots
     sources, held_in = refs[:loads], refs[3 + loads : 3 + 2 * loads]
     modulus, d_recv_0, d_recv_1 = refs[loads : 3 + loads]
     (
         z_send, z_recv, x_send, x_recv, w_send, w_recv, b_send, b_recv,
         s_send, s_recv, e_recv, t_send, t_recv, n_send, n_recv, m_recv,
-        tables, other, held, partial, back_hi, back_lo, lower, h_recv, c_send_0, c_send_1, c_recv_0, c_recv_1,
+        tables, other, held, image, partial, back_hi, back_lo, lower, h_recv, c_send_0, c_send_1, c_recv_0, c_recv_1,
         d_send_0, d_send_1,
         load_sem, send_sem, z_sem, x_sem, w_sem, b_sem, c_sem, d_sem, s_sem, h_sem,
     ) = refs[3 + 2 * loads :]
     (
-        spectrum, mirror_z, noise, ahead_hi, ahead_lo, mirror_x, mirror_y, y_hi, y_lo, x_ahead, x_back,
+        noise, ahead, spectrum, mirror_z, mirror_x, mirror_y, y_hi, y_lo, x_ahead, x_back,
         side_hi, side_lo, pool_rows, pool_columns, group_table,
     ) = held_in
 
@@ -254,7 +256,7 @@
     for peer in away_x:
         pl.semaphore_signal(barrier, inc=1, device_id={"px": peer}, device_id_type=MESH)
 
-    early = 6
+    early = 4
     for copy in copies[:early]:
         copy.start()
 
@@ -273,32 +275,9 @@
     d_routes = [route("py", d_send[f], d_recv[f], 14 + f, d_sem.at[f]) for f in range(members)]
 
     lane = lane_of((8, LANES))
+    quarter = (lane // 2) % slots
     half_y = ranks_y // 2
     my_half, my_place = me_y // half_y, me_y % half_y
-    copies[0].wait()
-    copies[1].wait()
-    mirrored = jnp.concatenate(
-        halves(spectrum[:, :, LANES : 2 * LANES].reshape(cells_x * cells_y, LANES)), 1
-    )
-    held[0, :, pl.ds(0, LANES)] = mm(mirrored, mirror_z[...])
-    for row in range(0, cells_y, 8):
-        rows = pl.ds(row, 8)
-        plain = [spectrum[x, rows, pl.ds(0, LANES)] for x in range(cells_x)]
-        turned_z = []
-        for x in range(cells_x):
-            value = held[0, pl.ds(x * cells_y + row, 8), pl.ds(0, LANES)]
-            turned_z.append(jnp.where(lane == 0, plain[x], value))
-        for kind, arrays in enumerate((plain, turned_z)):
-            moved = exchange(arrays, width)
-            for group in range(cells_x):
-                s_send[group % ranks_y, kind, group // ranks_y, rows] = moved[group]
-    strip = jnp.zeros((8, LANES), F32)
-    quarter = (lane // 2) % slots
-    for x in range(cells_x):
-        for part in range(cells_y // 8):
-            value = spectrum[x, pl.ds(part * 8, 8), pl.ds(LANES, 1)]
-            strip = jnp.where((lane // width == x) & (quarter == part), value, strip)
-    n_send[...] = strip
 
     def strip_copy():
         return pltpu.make_async_remote_copy(
@@ -334,45 +313,69 @@
     middle = (place == chips // 2) | (place == chips // 2 - 1)
     giver, taker = middle & (core == 0), middle & (core == 1)
 
-    def hand_copy(chunk):
+    def hand_copy(chunk, f):
         return pltpu.make_async_remote_copy(
-            src_ref=z_send.at[chunk, pl.ds((1 - my_half) * half_y, half_y)],
-            dst_ref=h_recv.at[chunk], send_sem=send_sem.at[0], recv_sem=h_sem.at[chunk],
+            src_ref=z_send.at[chunk, f, pl.ds((1 - my_half) * half_y, half_y)],
+            dst_ref=h_recv.at[chunk, f], send_sem=send_sem.at[0],
+            recv_sem=h_sem.at[chunk * members + f],
             device_id={"py": place * 2 + 1 - core}, device_id_type=MESH,
         )
 
-    def z_copy(source, chunk, slot, peer, send):
+    def z_copy(source, chunk, f, slot, peer, send):
         return pltpu.make_async_remote_copy(
-            src_ref=source, dst_ref=z_recv.at[chunk, slot], send_sem=send_sem.at[send],
-            recv_sem=z_sem.at[chunk], device_id={"py": peer}, device_id_type=MESH,
+            src_ref=source, dst_ref=z_recv.at[chunk, f, slot], send_sem=send_sem.at[send],
+            recv_sem=z_sem.at[chunk * members + f], device_id={"py": peer}, device_id_type=MESH,
         )
 
-    def z_start(chunk):
+    def z_start(chunk, f):
         @pl.when(giver)
         def _():
-            hand_copy(chunk).start()
+            hand_copy(chunk, f).start()
             for peer in others:
-                z_copy(z_send.at[chunk, peer], chunk, me_y, peer, 0).start()
+                z_copy(z_send.at[chunk, f, peer], chunk, f, me_y, peer, 0).start()
 
         @pl.when(jnp.logical_not(giver))
         def _():
-            z_route.start((chunk,), chunk)
+            z_route.start((chunk, f), chunk * members + f)
 
         @pl.when(taker)
         def _():
-            hand_copy(chunk).wait_recv()
+            hand_copy(chunk, f).wait_recv()
             for step, peer in enumerate(across):
-                z_copy(h_recv.at[chunk, step], chunk, me_y - 1, peer, 11).start()
-
-    for copy in copies[2:early]:
+                z_copy(h_recv.at[chunk, f, step], chunk, f, me_y - 1, peer, 11).start()
+
+    def own_spectrum():
+        mirrored = jnp.concatenate(
+            halves(spectrum[:, :, LANES : 2 * LANES].reshape(cells_x * cells_y, LANES)), 1
+        )
+        image[...] = mm(mirrored, mirror_z[...])
+        for row in range(0, cells_y, 8):
+            rows = pl.ds(row, 8)
+            plain = [spectrum[x, rows, pl.ds(0, LANES)] for x in range(cells_x)]
+            turned_z = []
+            for x in range(cells_x):
+                value = image[pl.ds(x * cells_y + row, 8)]
+                turned_z.append(jnp.where(lane == 0, plain[x], value))
+            for kind, arrays in enumerate((plain, turned_z)):
+                moved = exchange(arrays, width)
+                for group in range(cells_x):
+                    s_send[group % ranks_y, kind, group // ranks_y, rows] = moved[group]
+        strip = jnp.zeros((8, LANES), F32)
+        for x in range(cells_x):
+            for part in range(cells_y // 8):
+                value = spectrum[x, pl.ds(part * 8, 8), pl.ds(LANES, 1)]
+                strip = jnp.where((lane // width == x) & (quarter == part), value, strip)
+        n_send[...] = strip
+
+    for copy in copies[:2]:
         copy.wait()
-    for copy in copies[early:]:
-        copy.start()
     cells = cells_x * cells_y
-    for f in range(members):
-        high, low = halves(noise[f].reshape(cells, length_z))
-        held[f] = mm(high, ahead_hi[...]) + mm(high, ahead_lo[...]) + mm(low, ahead_hi[...])
+    lined = [halves(noise[f].reshape(cells, length_z)) for f in range(members)]
     for tile in range(tiles):
+        for f, (high, low) in enumerate(lined):
+            both = mm(high, ahead[tile])
+            both = both[:, :LANES] + both[:, LANES:] + mm(low, ahead[tile, :, pl.ds(0, LANES)])
+            held[f, :, pl.ds(tile * LANES, LANES)] = both
         lanes = pl.ds(tile * LANES, LANES)
         for row in range(0, cells_y, 8):
             rows = pl.ds(row, 8)
@@ -389,13 +392,18 @@
             for f in range(members):
                 for group in range(cells_x):
                     chunk = tile * per_tile + group // ranks_y
-                    z_send[chunk, group % ranks_y, f, rows] = both[f][group]
+                    z_send[chunk, f, group % ranks_y, rows] = both[f][group]
         if tile == 0:
             pl.semaphore_wait(barrier, ranks_y + slots - 2)
-            send_spectrum()
-        for part in range(per_tile):
-            chunk = tile * per_tile + part
-            z_start(chunk)
+        for part in range(tile * per_tile * members, (tile + 1) * per_tile * members):
+            z_start(part // members, part % members)
+            if part == 0:
+                for copy in copies[2:early]:
+                    copy.wait()
+                for copy in copies[early:]:
+                    copy.start()
+                own_spectrum()
+                send_spectrum()
 
     for copy in copies[early:]:
         copy.wait()
@@ -440,79 +448,59 @@
             recv_sem=s_sem.at[3], device_id={"px": 0}, device_id_type=MESH,
         )
 
-    def along_y(route, part, columns, ahead):
+    def along_y(columns):
         high, low = halves(columns)
-        product = mm(y_hi[...], high) + mm(y_hi[...], low) + mm(y_lo[...], high)
-        return product
-
-    def combined(product, f, start, rows, ahead):
-        lanes = slice(f * LANES, (f + 1) * LANES)
-        by_cos = product[start : start + rows, lanes]
-        by_sin = product[length_y + start : length_y + start + rows, lanes]
+        both = mm(y_hi[...], jnp.concatenate([high, low], 1))
+        return both[:, :LANES] + both[:, LANES:] + mm(y_lo[...], high)
+
+    def combined(product, start, rows, ahead):
+        by_cos = product[start : start + rows]
+        by_sin = product[length_y + start : length_y + start + rows]
         return by_cos + turned(by_sin, slots, ahead)
 
-    def y_ahead(chunk):
-        z_route.arrive((chunk,), chunk)
-        columns = [z_recv[chunk, :, f].reshape(length_y, LANES) for f in range(members)]
-        product = along_y(z_route, chunk, jnp.concatenate(columns, 1), True)
-        for part in range(parts):
-            for row in range(0, rows_part, 16):
-                arrays = []
-                for f in range(members):
-                    for block in range(blocks):
-                        at = block * rows_m + part * rows_part + row
-                        arrays.append(combined(product, f, at, 16, True))
-                moved = exchange(arrays, 1)
-                for rank in range(slots):
-                    x_send[chunk, part, rank, pl.ds(row, 16)] = moved[rank]
-            x_route.start((chunk, part), chunk * parts + part)
-
-    def gathered(ref, chunk, some):
+    def y_ahead(chunk, f):
+        part = chunk * members + f
+        z_route.arrive((chunk, f), part)
+        product = along_y(z_recv[chunk, f].reshape(length_y, LANES))
+        for row in range(0, rows_part, 16):
+            arrays = [combined(product, a * rows_part + row, 16, True) for a in range(slots)]
+            moved = exchange(arrays, 1)
+            for rank in range(slots):
+                x_send[chunk, f, rank, pl.ds(row, 16)] = moved[rank]
+        x_route.start((chunk, f), part)
+
+    def gathered(ref, chunk, f):
         pieces = [[] for _ in range(slots)]
-        for part in some:
-            for row in range(0, rows_part, 16):
-                moved = exchange([ref[chunk, part, s, pl.ds(row, 16)] for s in range(slots)], 1)
-                for index in range(slots):
-                    pieces[index].append(moved[index])
-        return [jnp.concatenate(piece, 0) for piece in pieces]
+        for row in range(0, rows_part, 16):
+            moved = exchange([ref[chunk, f, s, pl.ds(row, 16)] for s in range(slots)], 1)
+            for index in range(slots):
+                pieces[index].append(moved[index])
+        return jnp.concatenate([piece for some in pieces for piece in some], 0)
 
     def along_x(values, table):
         product = mm(jnp.concatenate(halves(values), 1), table[...])
         return product[:, :LANES] + product[:, LANES:]
 
-    def x_both(chunk):
-        for part in range(parts):
-            x_route.arrive((chunk, part), chunk * parts + part)
-            values = along_x(jnp.concatenate(gathered(x_recv, chunk, [part]), 0), x_ahead)
-            scaled = []
-            rows = pl.ds(part * rows_part, rows_part)
-            for f in range(members):
-                for block in range(blocks):
-                    at = (f * blocks + block) * rows_part
-                    table = other if f == 1 and chunk == 0 else tables.at[chunk]
-                    scaled.append(values[at : at + rows_part] * table[block, rows])
-            values = along_x(jnp.concatenate(scaled, 0), x_back)
-            for row in range(0, rows_part, 16):
-                arrays = [
-                    values[a * rows_part + row : a * rows_part + row + 16] for a in range(slots)
-                ]
-                moved = exchange(arrays, 1)
-                for s in range(slots):
-                    w_send[chunk, part, s, pl.ds(row, 16)] = moved[s]
-            w_route.start((chunk, part), chunk * parts + part)
-
-    def y_back(chunk):
-        for part in range(parts):
-            w_route.arrive((chunk, part), chunk * parts + part)
-        arrays = gathered(w_recv, chunk, range(parts))
-        columns = [
-            jnp.concatenate(arrays[f * blocks : (f + 1) * blocks], 0) for f in range(members)
-        ]
-        product = along_y(w_route, chunk, jnp.concatenate(columns, 1), False)
-        for f in range(members):
-            for p in range(ranks_y):
-                b_send[chunk, f, p] = combined(product, f, p * cells_y, cells_y, False)
-            b_route.start((chunk, f), chunk * members + f)
+    def x_both(chunk, f):
+        part = chunk * members + f
+        x_route.arrive((chunk, f), part)
+        table = other if part == 1 else tables.at[chunk]
+        values = along_x(gathered(x_recv, chunk, f), x_ahead)
+        values = along_x(values * table[...].reshape(length_y, LANES), x_back)
+        for row in range(0, rows_part, 16):
+            arrays = [values[a * rows_part + row : a * rows_part + row + 16] for a in range(slots)]
+            moved = exchange(arrays, 1)
+            for s in range(slots):
+                w_send[chunk, f, s, pl.ds(row, 16)] = moved[s]
+        w_route.start((chunk, f), part)
+
+    def y_back(chunk, f):
+        part = chunk * members + f
+        w_route.arrive((chunk, f), part)
+        product = along_y(gathered(w_recv, chunk, f))
+        for p in range(ranks_y):
+            b_send[chunk, f, p] = combined(product, p * cells_y, cells_y, False)
+        b_route.start((chunk, f), part)
 
     def table_rows(tile, block, rows, part):
         even = lane % 2 == 0
@@ -567,13 +555,16 @@
         n_recv[0] = n_send[...]
         pl.when(me_x != 0)(lambda: strips_copy(me_x).start())
 
-    y_ahead(0)
-    spectrum_tables()
-    for chunk in range(chunks):
-        x_both(chunk)
-        if chunk + 1 < chunks:
-            y_ahead(chunk + 1)
-        y_back(chunk)
+    steps = {"y": y_ahead, "x": x_both, "b": y_back}
+
+    def run(order):
+        for step in order:
+            if step == "T":
+                spectrum_tables()
+            else:
+                steps[step[0]](int(step[1:]) // members, int(step[1:]) % members)
+
+    run(ORDER)
 
     tall = cells // 4 // ranks_y
     def z_back(chunk, f):
@@ -645,7 +636,7 @@
         d_routes[f].arrive((), None)
 
     every = pl.ds(0, chunks)
-    z_route.drain((every,))
+    z_route.drain((every, pl.ds(0, members)))
 
     @pl.when(taker)
     def _():
@@ -654,8 +645,8 @@
             device_id={"py": others[0]}, device_id_type=MESH,
         ).wait_send()
 
-    x_route.drain((every, pl.ds(0, parts)))
-    w_route.drain((every, pl.ds(0, parts)))
+    x_route.drain((every, pl.ds(0, members)))
+    w_route.drain((every, pl.ds(0, members)))
     b_route.drain((every, pl.ds(0, members)))
     spot = s_send.at[pl.ds(0, half_y - 1)]
     pltpu.make_async_remote_copy(
@@ -683,12 +674,14 @@
     ranks_y, tall = first.shape[:2]
     copies = []
     for f, coarse in enumerate((first, second)):
-        copies.append(pltpu.make_async_copy(modulus.at[f], modulus_out.at[f], sems.at[f]))
-        copies.append(
-            pltpu.make_async_copy(
-                coarse.at[:, pl.ds(0, tall)], one_out.at[f], sems.at[members + f]
-            )
-        )
+        for x in range(0, cells_x, 2):
+            rows = pl.ds(x, 2)
+            copies.append((modulus.at[f, rows], modulus_out.at[f, rows]))
+        copies.append((coarse.at[:, pl.ds(0, tall)], one_out.at[f]))
+    copies = [
+        pltpu.make_async_copy(source, target, sems.at[index])
+        for index, (source, target) in enumerate(copies)
+    ]
     for copy in copies:
         copy.start()
     row = lax.broadcasted_iota(jnp.int32, (8, LANES), 0)
@@ -794,11 +787,15 @@
     pool_columns[z, LANES + z // 4] = 1.0
     pool_columns[z, LANES + length_z // 4 + z // 8] = 1.0
 
+    ahead = [
+        jnp.concatenate(host_halves(z_ahead[:, at : at + LANES]), 1)
+        for at in range(0, length_z, LANES)
+    ]
     held_in = [
+        white_noise,
+        jnp.stack(ahead),
         spectrum,
         jnp.asarray(np.tile(mirror_z, (2, 1)), BF16),
-        white_noise,
-        *host_halves(z_ahead),
         jnp.asarray(np.tile(mirror_x, (2, 1)), BF16),
         jnp.asarray(np.tile(mirror_y, (1, 2)), BF16),
         *host_halves(y_table),
@@ -818,8 +815,7 @@
     def vmem(*shape):
         return pltpu.VMEM(shape, F32)
 
-    z_shape = (chunks, size_py, members, cells_y, LANES)
-    x_shape = (chunks, PARTS, slots, rows_m // PARTS, LANES)
+    x_shape = (chunks, members, slots, length_y // slots, LANES)
     b_shape = (chunks, members, size_py, cells_y, LANES)
     s_shape = (2, tiles, cells_y, LANES)
     t_shape = (slots, rows_m, LANES)
@@ -828,7 +824,7 @@
     sem = pltpu.SemaphoreType.DMA
     scratch = [pltpu.VMEM(value.shape, value.dtype) for value in held_in[:-1]]
     scratch.append(pltpu.SMEM(group_table.shape, group_table.dtype))
-    for shape in (z_shape, x_shape, x_shape, b_shape):
+    for shape in (b_shape, x_shape, x_shape, b_shape):
         scratch += [vmem(*shape), vmem(*shape)]
     scratch += [vmem(size_py, *s_shape), vmem(size_py // 2, *s_shape), vmem(tiles, 8, LANES)]
     scratch += [vmem(*t_shape), vmem(*t_shape)]
@@ -837,16 +833,17 @@
         vmem(chunks, blocks, rows_m, LANES),
         vmem(blocks, rows_m, LANES),
         vmem(members, cells_x * cells_y, length_z),
+        vmem(cells_x * cells_y, LANES),
         vmem(members, half_cells, sides * length_z),
         pltpu.VMEM((chunks, 2 * LANES, sides * length_z), BF16),
         pltpu.VMEM((chunks, LANES, sides * length_z), BF16),
         vmem(size_py, 8, LANES),
-        vmem(chunks, size_py // 2, members, cells_y, LANES),
+        vmem(chunks, members, size_py // 2, cells_y, LANES),
         *[vmem(*shape) for shape in c_shapes * 3],
     ]
     scratch += [
-        sem((len(held_in),)), sem((16,)), sem((chunks,)), sem((chunks * PARTS,)),
-        sem((chunks * PARTS,)), sem((chunks * members,)), sem((members,)), sem((members,)), sem((5,)), sem((chunks,)),
+        sem((len(held_in),)), sem((16,)), sem((chunks * members,)), sem((chunks * members,)),
+        sem((chunks * members,)), sem((chunks * members,)), sem((members,)), sem((members,)), sem((5,)), sem((chunks * members,)),
     ]
     hbm = pl.BlockSpec(memory_space=pltpu.HBM)
     local = pl.BlockSpec(memory_space=pltpu.VMEM)
@@ -869,7 +866,7 @@
             out_shape=[jax.ShapeDtypeStruct(shape, F32) for shape in outs],
             in_specs=[local] * 3,
             out_specs=[hbm, hbm, local, local],
-            scratch_shapes=[sem((2 * members,))],
+            scratch_shapes=[sem((members * (cells_x // 2 + 1),))],
             compiler_params=pltpu.CompilerParams(vmem_limit_bytes=4 * 1024 * 1024),
         )(*leaving)
     )

time: 66.2 us -> 65 us (0.982)
  Pallas kernels: 65.2 us -> 64 us
    pallas_call x1, Pallas kernels: 63.6 us -> 62.3 us  [lanes_path(): pl.pallas_call(body, out_shape=[jax.ShapeDtypeStruct(shape, F32) for shap...]
where the time goes in v4:
time: 65 us; the launch traced here: 64.8 us
  Pallas kernels  64 us (98%)
  between operations  0.8 us (1%)
    pallas_call x1, Pallas kernels, lanes_path(): pl.pallas_call(body, out_shape=[jax.ShapeDtypeStruct(shape, F32) for shap...  62.3 us
    pallas_call x1, Pallas kernels, lanes_path(): pl.pallas_call(leaving_kernel, out_shape=[jax.ShapeDtypeStruct(shape, F32...  1.77 us

profile of v4, /device:TPU:0, one launch (start us, length us, event | category | flops | bytes accessed | tf_op | source)
XLA Modules:
  0.0 64.8 jit_solution(1949928324278475856)
XLA Ops:
  0.6 62.3 %shard_map.219 = (f32[2,16,32,256]{3,2,1,0:T(8,128)S(1)}, f32[8,16,128]{2,1,0:T(8,128)S(1)}, f32[8,24,128]{2,1,0:T(8,128)S(1)}) custom-call(f32[2,16,32,256]{3,2,1,0:T(8,128)} %refs_0_.1, bf16[2,256,256]{2,1,0:T(8,128)(2,1)} %constant.61.refs_1_, f32[16,32,256]{2,1,0:T(8,128)} %refs_2_.1, bf16[256,128]{1,0:T(8,128)(2,1)} %constant.42.clone.refs_3_, ...), custom_call_target="tpu_custom_call" | custom-call | tf_op jit(solution)/shard_map/pallas_call | solution.py:850
  62.9 1.8 %shard_map.220 = (f32[2,16,32,256]{3,2,1,0:T(8,128)}, f32[2,8,16,128]{3,2,1,0:T(8,128)}, f32[2,4,8,64]{3,2,1,0:T(8,128)}, f32[2,2,4,32]{3,2,1,0:T(4,128)}) custom-call(f32[2,16,32,256]{3,2,1,0:T(8,128)S(1)} %get-tuple-element.7.modulus, f32[8,16,128]{2,1,0:T(8,128)S(1)} %get-tuple-element.8.first, f32[8,24,128]{2,1,0:T(8,128)S(1)} %get-tuple-element.9.second), custom_call_target="tpu_custom_call" | custom-call | tf_op jit(solution)/shard_map/pallas_call | solution.py:864

commit v5 on v4

--- a/solution.py
+++ b/solution.py
@@ -225,9 +225,9 @@
     (
         z_send, z_recv, x_send, x_recv, w_send, w_recv, b_send, b_recv,
         s_send, s_recv, e_recv, t_send, t_recv, n_send, n_recv, m_recv,
-        tables, other, held, image, partial, back_hi, back_lo, lower, h_recv, c_send_0, c_send_1, c_recv_0, c_recv_1,
+        tables, other, held, image, partial, back_hi, back_lo, h_recv, g_recv, c_send_0, c_send_1, c_recv_0, c_recv_1,
         d_send_0, d_send_1,
-        load_sem, send_sem, z_sem, x_sem, w_sem, b_sem, c_sem, d_sem, s_sem, h_sem,
+        load_sem, send_sem, z_sem, x_sem, w_sem, b_sem, c_sem, d_sem, s_sem, h_sem, g_sem,
     ) = refs[3 + 2 * loads :]
     (
         noise, ahead, spectrum, mirror_z, mirror_x, mirror_y, y_hi, y_lo, x_ahead, x_back,
@@ -235,9 +235,11 @@
     ) = held_in
 
     me_x, me_y = lax.axis_index("px"), lax.axis_index("py")
+    pairs = [(sources[0].at[f], noise.at[f]) for f in range(members)]
+    pairs = [pairs[0], (sources[1], ahead), *pairs[1:], *list(zip(sources, held_in))[2:]]
     copies = [
         pltpu.make_async_copy(source, target, load_sem.at[index])
-        for index, (source, target) in enumerate(zip(sources, held_in))
+        for index, (source, target) in enumerate(pairs)
     ]
     place, core = me_y // 2, me_y % 2
     chips = ranks_y // 2
@@ -256,7 +258,7 @@
     for peer in away_x:
         pl.semaphore_signal(barrier, inc=1, device_id={"px": peer}, device_id_type=MESH)
 
-    early = 4
+    early = 5
     for copy in copies[:early]:
         copy.start()
 
@@ -313,36 +315,40 @@
     middle = (place == chips // 2) | (place == chips // 2 - 1)
     giver, taker = middle & (core == 0), middle & (core == 1)
 
-    def hand_copy(chunk, f):
-        return pltpu.make_async_remote_copy(
-            src_ref=z_send.at[chunk, f, pl.ds((1 - my_half) * half_y, half_y)],
-            dst_ref=h_recv.at[chunk, f], send_sem=send_sem.at[0],
-            recv_sem=h_sem.at[chunk * members + f],
-            device_id={"py": place * 2 + 1 - core}, device_id_type=MESH,
-        )
-
-    def z_copy(source, chunk, f, slot, peer, send):
-        return pltpu.make_async_remote_copy(
-            src_ref=source, dst_ref=z_recv.at[chunk, f, slot], send_sem=send_sem.at[send],
-            recv_sem=z_sem.at[chunk * members + f], device_id={"py": peer}, device_id_type=MESH,
-        )
-
-    def z_start(chunk, f):
+    def shared_start(route, where, part, hand, hand_sem, extra):
+        source, target = route.source, route.target
+        blocks_away = source.at[where + (pl.ds((1 - my_half) * half_y, half_y),)]
+
+        def hand_copy():
+            return pltpu.make_async_remote_copy(
+                src_ref=blocks_away, dst_ref=hand, send_sem=route.send, recv_sem=hand_sem,
+                device_id={"py": place * 2 + 1 - core}, device_id_type=MESH,
+            )
+
         @pl.when(giver)
         def _():
-            hand_copy(chunk, f).start()
+            hand_copy().start()
             for peer in others:
-                z_copy(z_send.at[chunk, f, peer], chunk, f, me_y, peer, 0).start()
+                spot = source.at[where + (peer,)]
+                route.copy(spot, target.at[where + (me_y,)], peer, part).start()
 
         @pl.when(jnp.logical_not(giver))
         def _():
-            z_route.start((chunk, f), chunk * members + f)
+            route.start(where, part)
 
         @pl.when(taker)
         def _():
-            hand_copy(chunk, f).wait_recv()
+            hand_copy().wait_recv()
             for step, peer in enumerate(across):
-                z_copy(h_recv.at[chunk, f, step], chunk, f, me_y - 1, peer, 11).start()
+                pltpu.make_async_remote_copy(
+                    src_ref=hand.at[step], dst_ref=target.at[where + (me_y - 1,)],
+                    send_sem=send_sem.at[extra], recv_sem=route.recv.at[part],
+                    device_id={"py": peer}, device_id_type=MESH,
+                ).start()
+
+    def z_start(chunk, f):
+        part = chunk * members + f
+        shared_start(z_route, (chunk, f), part, h_recv.at[chunk, f], h_sem.at[part], 11)
 
     def own_spectrum():
         mirrored = jnp.concatenate(
@@ -367,12 +373,15 @@
                 strip = jnp.where((lane // width == x) & (quarter == part), value, strip)
         n_send[...] = strip
 
-    for copy in copies[:2]:
-        copy.wait()
     cells = cells_x * cells_y
-    lined = [halves(noise[f].reshape(cells, length_z)) for f in range(members)]
+    lined = []
     for tile in range(tiles):
-        for f, (high, low) in enumerate(lined):
+        for f in range(members):
+            if tile == 0:
+                for copy in copies[2 * f : 2 + f]:
+                    copy.wait()
+                lined.append(halves(noise[f].reshape(cells, length_z)))
+            high, low = lined[f]
             both = mm(high, ahead[tile])
             both = both[:, :LANES] + both[:, LANES:] + mm(low, ahead[tile, :, pl.ds(0, LANES)])
             held[f, :, pl.ds(tile * LANES, LANES)] = both
@@ -398,7 +407,7 @@
         for part in range(tile * per_tile * members, (tile + 1) * per_tile * members):
             z_start(part // members, part % members)
             if part == 0:
-                for copy in copies[2:early]:
+                for copy in copies[3:early]:
                     copy.wait()
                 for copy in copies[early:]:
                     copy.start()
@@ -500,7 +509,11 @@
         product = along_y(gathered(w_recv, chunk, f))
         for p in range(ranks_y):
             b_send[chunk, f, p] = combined(product, p * cells_y, cells_y, False)
-        b_route.start((chunk, f), part)
+        late = part - (chunks * members - g_recv.shape[0])
+        if late >= 0:
+            shared_start(b_route, (chunk, f), part, g_recv.at[late], g_sem.at[late], 7)
+        else:
+            b_route.start((chunk, f), part)
 
     def table_rows(tile, block, rows, part):
         even = lane % 2 == 0
@@ -590,7 +603,9 @@
             lanes = slice(side * length_z, (side + 1) * length_z)
             cut = values[:, lanes].reshape(ranks_y, cells_y, length_z)
             modulus[f, pl.ds(side * ranks_y, ranks_y)] = cut
-        high, low = halves(values)
+        paired = values.reshape(ranks_y // 2, 2, cells_y, sides * length_z)
+        paired = (paired[:, 0] + paired[:, 1]).reshape(-1, sides * length_z)
+        high, low = halves(paired)
         pooled = mm(pool_rows[...], high) + mm(pool_rows[...], low)
         pooled = [pooled[:, side * length_z : (side + 1) * length_z] for side in range(sides)]
         high, low = halves(jnp.concatenate(pooled, 0))
@@ -604,22 +619,16 @@
             at = base + per_side * tall + d % per_side * 8
             value = coarse[at : at + 8, LANES:]
             value = jnp.where(lane < LANES // 2, value, pltpu.roll(value, 4, 0))
-            if f == 0:
-                lower[d] = value
-            else:
-                c_send[f][d, pl.ds(tall, 8)] = jnp.where(
-                    sublane < 4, lower[d], pltpu.roll(value, 4, 0)
-                )
+            c_send[f][d, pl.ds(tall, 4)] = value[:4]
         c_routes[f].start((), None)
 
     def pick(f):
         c_routes[f].arrive((), None)
         for g in range(ranks_y):
             d_send[f][g, pl.ds(0, tall)] = c_recv[f][group_table[0, g], pl.ds(0, tall)]
-            if f == 1:
-                second = c_recv[f][group_table[1, g], pl.ds(tall, 8)]
-                third = c_recv[f][group_table[2, g], pl.ds(tall, 8)]
-                d_send[f][g, pl.ds(tall, 8)] = jnp.where(lane < LANES // 2, second, third)
+            second = c_recv[f][group_table[1, g], pl.ds(tall, 4)]
+            third = c_recv[f][group_table[2, g], pl.ds(tall, 4)]
+            d_send[f][g, pl.ds(tall, 4)] = jnp.where(lane[:4] < LANES // 2, second, third)
         d_routes[f].start((), None)
 
     for chunk in range(chunks):
@@ -644,6 +653,10 @@
             src_ref=h_recv, dst_ref=h_recv, send_sem=send_sem.at[11], recv_sem=h_sem.at[0],
             device_id={"py": others[0]}, device_id_type=MESH,
         ).wait_send()
+        pltpu.make_async_remote_copy(
+            src_ref=g_recv, dst_ref=g_recv, send_sem=send_sem.at[7], recv_sem=g_sem.at[0],
+            device_id={"py": others[0]}, device_id_type=MESH,
+        ).wait_send()
 
     x_route.drain((every, pl.ds(0, members)))
     w_route.drain((every, pl.ds(0, members)))
@@ -669,14 +682,13 @@
     pl.when((me_y == 0) & (me_x != 0))(lambda: strips_copy(me_x).wait_send())
 
 
-def leaving_kernel(modulus, first, second, modulus_out, one_out, level_two, level_three, sems):
+def leaving_kernel(modulus, first, second, *refs):
+    modulus_out, one_out, two_out, three_out, level_two, level_three, sems = refs
     members, cells_x, cells_y, length_z = modulus.shape
-    ranks_y, tall = first.shape[:2]
+    ranks_y, tall = first.shape[0], first.shape[1] - 4
     copies = []
     for f, coarse in enumerate((first, second)):
-        for x in range(0, cells_x, 2):
-            rows = pl.ds(x, 2)
-            copies.append((modulus.at[f, rows], modulus_out.at[f, rows]))
+        copies.append((modulus.at[f], modulus_out.at[f]))
         copies.append((coarse.at[:, pl.ds(0, tall)], one_out.at[f]))
     copies = [
         pltpu.make_async_copy(source, target, sems.at[index])
@@ -684,27 +696,16 @@
     ]
     for copy in copies:
         copy.start()
-    row = lax.broadcasted_iota(jnp.int32, (8, LANES), 0)
-    short = cells_y // 4
-    lows = [second[d, pl.ds(tall, 8)] for d in range(ranks_y)]
-    for f in range(members):
-        shifts = [4 * f, 4 - 4 * f]
-        for x in range(ranks_y // 2):
-            pair = [
-                pltpu.roll(low, shift, 0) if shift else low
-                for low, shift in zip(lows[2 * x : 2 * x + 2], shifts)
-            ]
-            value = jnp.where(row < 4, *pair)
-            level_two[f, x] = value[:short, : length_z // 4]
-        for x in range(ranks_y // 4):
-            value = jnp.zeros((8, LANES), F32)
-            for y in range(4):
-                low = lows[4 * x + y]
-                shift = (y - 4 * f) % 8
-                low = pltpu.roll(low, shift, 0) if shift else low
-                value = jnp.where(row == y, low, value)
-            value = pltpu.roll(value, LANES // 2, 1)
-            level_three[f, x] = value[: short // 2, : length_z // 8]
+    wide, narrow = level_two.shape[3], level_three.shape[3]
+    for f, coarse in enumerate((first, second)):
+        for d in range(ranks_y):
+            low = coarse[d, pl.ds(tall, 4)]
+            level_two[f, d // 2, pl.ds(d % 2 * 4, 4)] = low[:, :wide]
+            low = pltpu.roll(low, LANES // 2, 1)
+            level_three[f, d // 4, pl.ds(d % 4, 1)] = low[:1, :narrow]
+    for level, out in ((level_two, two_out), (level_three, three_out)):
+        copies.append(pltpu.make_async_copy(level, out, sems.at[len(copies)]))
+        copies[-1].start()
     for copy in copies:
         copy.wait()
 
@@ -769,15 +770,15 @@
     mirror_x = np.where(same & (mode[0][:, None] == mode[0][None]), 1.0, 0.0)
 
     def pool(extent_x, extent_y, factor):
-        short_x, short_y = extent_x // factor, extent_y // factor
+        short_x, short_y = 2 * extent_x // factor, extent_y // factor
         row, cell = np.arange(short_x * short_y), np.arange(extent_x * extent_y)
-        same_x = cell[None] // extent_y // factor == row[:, None] // short_y
+        same_x = cell[None] // extent_y // (factor // 2) == row[:, None] // short_y
         same_y = cell[None] % extent_y // factor == row[:, None] % short_y
         return np.where(same_x & same_y, 1.0 / factor**3, 0.0)
 
     per_side = size_py // sides
-    some = size_py, cells_y
-    lower = np.zeros((per_side, 8, half_cells))
+    some = size_py // 2, cells_y
+    lower = np.zeros((per_side, 8, half_cells // 2))
     lower[:, :4] = pool(*some, 4).reshape(per_side, 4, -1)
     lower[:, 4:5] = pool(*some, 8).reshape(per_side, 1, -1)
     pool_rows = np.concatenate([pool(*some, 2), lower.reshape(8 * per_side, -1)], 0)
@@ -820,7 +821,7 @@
     s_shape = (2, tiles, cells_y, LANES)
     t_shape = (slots, rows_m, LANES)
     tall = cells_x * cells_y // 4 // size_py
-    c_shapes = [(size_py, tall, LANES), (size_py, tall + 8, LANES)]
+    c_shapes = [(size_py, tall + 4, LANES)] * members
     sem = pltpu.SemaphoreType.DMA
     scratch = [pltpu.VMEM(value.shape, value.dtype) for value in held_in[:-1]]
     scratch.append(pltpu.SMEM(group_table.shape, group_table.dtype))
@@ -837,13 +838,13 @@
         vmem(members, half_cells, sides * length_z),
         pltpu.VMEM((chunks, 2 * LANES, sides * length_z), BF16),
         pltpu.VMEM((chunks, LANES, sides * length_z), BF16),
-        vmem(size_py, 8, LANES),
         vmem(chunks, members, size_py // 2, cells_y, LANES),
+        vmem(members, size_py // 2, cells_y, LANES),
         *[vmem(*shape) for shape in c_shapes * 3],
     ]
     scratch += [
-        sem((len(held_in),)), sem((16,)), sem((chunks * members,)), sem((chunks * members,)),
-        sem((chunks * members,)), sem((chunks * members,)), sem((members,)), sem((members,)), sem((5,)), sem((chunks * members,)),
+        sem((len(held_in) + 1,)), sem((16,)), sem((chunks * members,)), sem((chunks * members,)),
+        sem((chunks * members,)), sem((chunks * members,)), sem((members,)), sem((members,)), sem((5,)), sem((chunks * members,)), sem((members,)),
     ]
     hbm = pl.BlockSpec(memory_space=pltpu.HBM)
     local = pl.BlockSpec(memory_space=pltpu.VMEM)
@@ -865,8 +866,8 @@
             leaving_kernel,
             out_shape=[jax.ShapeDtypeStruct(shape, F32) for shape in outs],
             in_specs=[local] * 3,
-            out_specs=[hbm, hbm, local, local],
-            scratch_shapes=[sem((members * (cells_x // 2 + 1),))],
+            out_specs=[hbm] * 4,
+            scratch_shapes=[vmem(*outs[2]), vmem(*outs[3]), sem((2 * members + 2,))],
             compiler_params=pltpu.CompilerParams(vmem_limit_bytes=4 * 1024 * 1024),
         )(*leaving)
     )

time: 65 us -> 63.8 us (0.982)
  Pallas kernels: 64 us -> 62.8 us
    pallas_call x1, Pallas kernels: 1.77 us -> 1.06 us  [lanes_path(): pl.pallas_call(leaving_kernel, out_shape=[jax.ShapeDtypeStruct(shape, F32...]
where the time goes in v5:
time: 63.8 us; the launch traced here: 63.6 us
  Pallas kernels  62.8 us (98%)
  between operations  0.8 us (1%)
    pallas_call x1, Pallas kernels, lanes_path(): pl.pallas_call(body, out_shape=[jax.ShapeDtypeStruct(shape, F32) for shap...  61.7 us

profile of v5, /device:TPU:0, one launch (start us, length us, event | category | flops | bytes accessed | tf_op | source)
XLA Modules:
  0.0 63.6 jit_solution(9519701168178188861)
XLA Ops:
  0.6 61.7 %shard_map.219 = (f32[2,16,32,256]{3,2,1,0:T(8,128)S(1)}, f32[8,20,128]{2,1,0:T(8,128)S(1)}, f32[8,20,128]{2,1,0:T(8,128)S(1)}) custom-call(f32[2,16,32,256]{3,2,1,0:T(8,128)} %refs_0_.1, bf16[2,256,256]{2,1,0:T(8,128)(2,1)} %constant.61.refs_1_, f32[16,32,256]{2,1,0:T(8,128)} %refs_2_.1, bf16[256,128]{1,0:T(8,128)(2,1)} %constant.42.clone.refs_3_, ...), custom_call_target="tpu_custom_call" | custom-call | tf_op jit(solution)/shard_map/pallas_call | solution.py:851
  62.4 1.1 %shard_map.220 = (f32[2,16,32,256]{3,2,1,0:T(8,128)}, f32[2,8,16,128]{3,2,1,0:T(8,128)}, f32[2,4,8,64]{3,2,1,0:T(8,128)}, f32[2,2,4,32]{3,2,1,0:T(4,128)}) custom-call(f32[2,16,32,256]{3,2,1,0:T(8,128)S(1)} %get-tuple-element.7.modulus, f32[8,20,128]{2,1,0:T(8,128)S(1)} %get-tuple-element.8.first, f32[8,20,128]{2,1,0:T(8,128)S(1)} %get-tuple-element.9.second), custom_call_target="tpu_custom_call" | custom-call | tf_op jit(solution)/shard_map/pallas_call | solution.py:865

commit v6 on v5

--- a/solution.py
+++ b/solution.py
@@ -225,13 +225,13 @@
     (
         z_send, z_recv, x_send, x_recv, w_send, w_recv, b_send, b_recv,
         s_send, s_recv, e_recv, t_send, t_recv, n_send, n_recv, m_recv,
-        tables, other, held, image, partial, back_hi, back_lo, h_recv, g_recv, c_send_0, c_send_1, c_recv_0, c_recv_1,
+        tables, other, held, image, partial, h_recv, g_recv, c_send_0, c_send_1, c_recv_0, c_recv_1,
         d_send_0, d_send_1,
         load_sem, send_sem, z_sem, x_sem, w_sem, b_sem, c_sem, d_sem, s_sem, h_sem, g_sem,
     ) = refs[3 + 2 * loads :]
     (
         noise, ahead, spectrum, mirror_z, mirror_x, mirror_y, y_hi, y_lo, x_ahead, x_back,
-        side_hi, side_lo, pool_rows, pool_columns, group_table,
+        back, pool_rows, pool_columns, group_table,
     ) = held_in
 
     me_x, me_y = lax.axis_index("px"), lax.axis_index("py")
@@ -244,7 +244,9 @@
     place, core = me_y // 2, me_y % 2
     chips = ranks_y // 2
     near = chips - 1 - (chips - 2) * (place % 2)
-    steps = [chips // 2, near, chips - near]
+    inner = (place + 1) // 2 % 2
+    far = near - (near - chips // 2) * inner
+    steps = [far, near + chips // 2 - far, chips - near]
     away_y = []
     for step in steps:
         for side in (0, 1):
@@ -295,12 +297,13 @@
 
     def edge_copy(peer):
         return pltpu.make_async_remote_copy(
-            src_ref=s_send.at[peer, 1, :, pl.ds(0, 8)], dst_ref=e_recv, send_sem=send_sem.at[10],
+            src_ref=s_send.at[peer, 1, :, pl.ds(0, 1)], dst_ref=e_recv, send_sem=send_sem.at[10],
             recv_sem=s_sem.at[4], device_id={"py": peer}, device_id_type=MESH,
         )
 
     others = [my_half * half_y + (my_place + step) % half_y for step in range(1, half_y)]
-    across = [(1 - my_half) * half_y + step for step in range(half_y)]
+    places = [(step + half_y // 2 * (1 - my_half)) % half_y for step in range(half_y)]
+    across = [(1 - my_half) * half_y + spot for spot in places]
 
     def send_spectrum():
         pl.when(me_y != 0)(lambda: strip_copy().start())
@@ -339,9 +342,9 @@
         @pl.when(taker)
         def _():
             hand_copy().wait_recv()
-            for step, peer in enumerate(across):
+            for spot, peer in zip(places, across):
                 pltpu.make_async_remote_copy(
-                    src_ref=hand.at[step], dst_ref=target.at[where + (me_y - 1,)],
+                    src_ref=hand.at[spot], dst_ref=target.at[where + (me_y - 1,)],
                     send_sem=send_sem.at[extra], recv_sem=route.recv.at[part],
                     device_id={"py": peer}, device_id_type=MESH,
                 ).start()
@@ -417,15 +420,6 @@
     for copy in copies[early:]:
         copy.wait()
     sides = cells_x // ranks_y
-    rows_side = LANES // sides
-    for target, source, count in ((back_hi, side_hi, 2), (back_lo, side_lo, 1)):
-        blank = jnp.zeros((rows_side, length_z), BF16)
-        for chunk in range(chunks):
-            for block in range(count * sides):
-                rows = pl.ds(block * rows_side, rows_side)
-                for side in range(sides):
-                    value = source[chunk] if block % sides == side else blank
-                    target[chunk, rows, pl.ds(side * length_z, length_z)] = value
 
     spot = s_recv.at[pl.ds(0, half_y - 1)]
     pltpu.make_async_remote_copy(
@@ -591,36 +585,49 @@
             moved = exchange(arrays, width)
             for x in range(ranks_y):
                 pieces[x].append(moved[x])
-        high, low = halves(jnp.concatenate([piece for some in pieces for piece in some], 0))
-        fields = mm(jnp.concatenate([high, low], 1), back_hi[chunk]) + mm(high, back_lo[chunk])
-        if chunk > 0:
-            fields = fields + partial[f]
+        cells_by = jnp.concatenate([piece for some in pieces for piece in some], 0)
+        swapped = pltpu.roll(cells_by, LANES // 2, 1)
+        near_side = lane_of(cells_by.shape) < LANES // 2
+        first_side = 0 if chunk + 1 < chunks else 1 - my_half
+        if chunk + 1 == chunks:
+            flip = first_side == 1
+            cells_by, swapped = (
+                jnp.where(flip, swapped, cells_by), jnp.where(flip, cells_by, swapped)
+            )
+
+        def fields(value, beside, side):
+            high = value.astype(BF16)
+            low = beside - beside.astype(BF16).astype(F32)
+            mixed = jnp.where(near_side, high.astype(F32), low).astype(BF16)
+            result = mm(jnp.concatenate([mixed, high], 1), back[chunk])
+            return result + partial[f, side] if chunk > 0 else result
+
         if chunk + 1 < chunks:
-            partial[f] = fields
+            partial[f, 0] = fields(cells_by, swapped, 0)
+            partial[f, 1] = fields(swapped, cells_by, 1)
             return
-        values = jnp.exp(0.5 * fields)
-        for side in range(sides):
-            lanes = slice(side * length_z, (side + 1) * length_z)
-            cut = values[:, lanes].reshape(ranks_y, cells_y, length_z)
+        for side, peers, value, beside in (
+            (1 - my_half, across, cells_by, swapped), (my_half, others, swapped, cells_by)
+        ):
+            values = jnp.exp2(fields(value, beside, side))
+            cut = values.reshape(ranks_y, cells_y, length_z)
             modulus[f, pl.ds(side * ranks_y, ranks_y)] = cut
-        paired = values.reshape(ranks_y // 2, 2, cells_y, sides * length_z)
-        paired = (paired[:, 0] + paired[:, 1]).reshape(-1, sides * length_z)
-        high, low = halves(paired)
-        pooled = mm(pool_rows[...], high) + mm(pool_rows[...], low)
-        pooled = [pooled[:, side * length_z : (side + 1) * length_z] for side in range(sides)]
-        high, low = halves(jnp.concatenate(pooled, 0))
-        coarse = mm(high, pool_columns[...]) + mm(low, pool_columns[...])
-        per_side = ranks_y // sides
-        height = coarse.shape[0] // sides
-        for d in range(ranks_y):
-            base = d // per_side * height
-            at = base + d % per_side * tall
-            c_send[f][d, pl.ds(0, tall)] = coarse[at : at + tall, :LANES]
-            at = base + per_side * tall + d % per_side * 8
-            value = coarse[at : at + 8, LANES:]
-            value = jnp.where(lane < LANES // 2, value, pltpu.roll(value, 4, 0))
-            c_send[f][d, pl.ds(tall, 4)] = value[:4]
-        c_routes[f].start((), None)
+            paired = values.reshape(ranks_y // 2, 2, cells_y, length_z)
+            paired = (paired[:, 0] + paired[:, 1]).reshape(-1, length_z)
+            high_part, low_part = halves(paired)
+            pooled = mm(pool_rows[...], jnp.concatenate([high_part, low_part], 0))
+            high_part, low_part = halves(pooled)
+            coarse = mm(high_part, pool_columns[...]) + mm(low_part, pool_columns[...])
+            for e in range(half_y):
+                piece = side * half_y + e
+                c_send[f][piece, pl.ds(0, tall)] = coarse[e * tall : (e + 1) * tall, :LANES]
+                at = half_y * tall + e * 8
+                value = coarse[at : at + 8, LANES:]
+                value = jnp.where(lane < LANES // 2, value, pltpu.roll(value, 4, 0))
+                c_send[f][piece, pl.ds(tall, 4)] = value[:4]
+            for peer in peers:
+                spot = c_recv[f].at[me_y]
+                c_routes[f].copy(c_send[f].at[peer], spot, peer, None).start()
 
     def pick(f):
         c_routes[f].arrive((), None)
@@ -669,7 +676,7 @@
 
     @pl.when(my_place == 0)
     def _():
-        spot = s_send.at[pl.ds(0, half_y), 1, :, pl.ds(0, 8)]
+        spot = s_send.at[pl.ds(0, half_y), 1, :, pl.ds(0, 1)]
         pltpu.make_async_remote_copy(
             src_ref=spot, dst_ref=spot, send_sem=send_sem.at[10], recv_sem=s_sem.at[4],
             device_id={"py": others[0]}, device_id_type=MESH,
@@ -736,11 +743,12 @@
     z_ahead[:, second] = sign[:, None]
     z_back[:, first] = 1.0
     z_back[:, second] = sign[:, None]
-    z_back = z_back.T / (length_x * length_y * length_z)
+    z_back = z_back.T * (0.5 / np.log(2.0) / (length_x * length_y * length_z))
 
     sides = cells_x // size_py
     half_cells = cells_x * cells_y // sides
     back_hi, back_lo = host_halves(z_back.reshape(chunks, LANES // sides, length_z))
+    back = jnp.concatenate([back_hi, back_hi, back_lo, jnp.zeros_like(back_lo)], 1)
 
     angles = angles_of(length_y)
     y_table = np.concatenate([np.cos(angles), np.sin(angles)], 0)
@@ -802,9 +810,8 @@
         *host_halves(y_table),
         x_table(-1.0, cell, mode),
         x_table(1.0, mode, cell),
-        back_hi,
-        back_lo,
-        jnp.asarray(pool_rows, BF16),
+        back,
+        jnp.asarray(np.tile(pool_rows, (1, 2)), BF16),
         jnp.asarray(pool_columns, BF16),
         group_table,
     ]
@@ -827,7 +834,7 @@
     scratch.append(pltpu.SMEM(group_table.shape, group_table.dtype))
     for shape in (b_shape, x_shape, x_shape, b_shape):
         scratch += [vmem(*shape), vmem(*shape)]
-    scratch += [vmem(size_py, *s_shape), vmem(size_py // 2, *s_shape), vmem(tiles, 8, LANES)]
+    scratch += [vmem(size_py, *s_shape), vmem(size_py // 2, *s_shape), vmem(tiles, 1, LANES)]
     scratch += [vmem(*t_shape), vmem(*t_shape)]
     scratch += [vmem(8, LANES), vmem(size_py, 8, LANES), vmem(slots, size_py, 8, LANES)]
     scratch += [
@@ -835,9 +842,7 @@
         vmem(blocks, rows_m, LANES),
         vmem(members, cells_x * cells_y, length_z),
         vmem(cells_x * cells_y, LANES),
-        vmem(members, half_cells, sides * length_z),
-        pltpu.VMEM((chunks, 2 * LANES, sides * length_z), BF16),
-        pltpu.VMEM((chunks, LANES, sides * length_z), BF16),
+        vmem(members, sides, half_cells, length_z),
         vmem(chunks, members, size_py // 2, cells_y, LANES),
         vmem(members, size_py // 2, cells_y, LANES),
         *[vmem(*shape) for shape in c_shapes * 3],

time: 63.8 us -> 63.7 us (level)
  no operation moved by 1% of the time
where the time goes in v6:
time: 63.7 us; the launch traced here: 63.5 us
  Pallas kernels  62.7 us (98%)
  between operations  0.8 us (1%)
    pallas_call x1, Pallas kernels, lanes_path(): pl.pallas_call(body, out_shape=[jax.ShapeDtypeStruct(shape, F32) for shap...  61.7 us

profile of v6, /device:TPU:0, one launch (start us, length us, event | category | flops | bytes accessed | tf_op | source)
XLA Modules:
  0.0 63.5 jit_solution(6671965874481426714)
XLA Ops:
  0.6 61.7 %shard_map.219 = (f32[2,16,32,256]{3,2,1,0:T(8,128)S(1)}, f32[8,20,128]{2,1,0:T(8,128)S(1)}, f32[8,20,128]{2,1,0:T(8,128)S(1)}) custom-call(f32[2,16,32,256]{3,2,1,0:T(8,128)} %refs_0_.1, bf16[2,256,256]{2,1,0:T(8,128)(2,1)} %constant.62.refs_1_, f32[16,32,256]{2,1,0:T(8,128)} %refs_2_.1, bf16[256,128]{1,0:T(8,128)(2,1)} %constant.43.clone.refs_3_, ...), custom_call_target="tpu_custom_call" | custom-call | tf_op jit(solution)/shard_map/pallas_call | solution.py:856
  62.3 1.1 %shard_map.220 = (f32[2,16,32,256]{3,2,1,0:T(8,128)}, f32[2,8,16,128]{3,2,1,0:T(8,128)}, f32[2,4,8,64]{3,2,1,0:T(8,128)}, f32[2,2,4,32]{3,2,1,0:T(4,128)}) custom-call(f32[2,16,32,256]{3,2,1,0:T(8,128)S(1)} %get-tuple-element.7.modulus, f32[8,20,128]{2,1,0:T(8,128)S(1)} %get-tuple-element.8.first, f32[8,20,128]{2,1,0:T(8,128)S(1)} %get-tuple-element.9.second), custom_call_target="tpu_custom_call" | custom-call | tf_op jit(solution)/shard_map/pallas_call | solution.py:870

commit v7 on v6

--- a/solution.py
+++ b/solution.py
@@ -844,12 +844,12 @@
         vmem(cells_x * cells_y, LANES),
         vmem(members, sides, half_cells, length_z),
         vmem(chunks, members, size_py // 2, cells_y, LANES),
-        vmem(members, size_py // 2, cells_y, LANES),
+        vmem(2 * members, size_py // 2, cells_y, LANES),
         *[vmem(*shape) for shape in c_shapes * 3],
     ]
     scratch += [
         sem((len(held_in) + 1,)), sem((16,)), sem((chunks * members,)), sem((chunks * members,)),
-        sem((chunks * members,)), sem((chunks * members,)), sem((members,)), sem((members,)), sem((5,)), sem((chunks * members,)), sem((members,)),
+        sem((chunks * members,)), sem((chunks * members,)), sem((members,)), sem((members,)), sem((5,)), sem((chunks * members,)), sem((2 * members,)),
     ]
     hbm = pl.BlockSpec(memory_space=pltpu.HBM)
     local = pl.BlockSpec(memory_space=pltpu.VMEM)

time: 63.7 us -> 63.7 us (level)
  no operation moved by 1% of the time
where the time goes in v7:
time: 63.7 us; the launch traced here: 63.6 us
  Pallas kernels  62.8 us (99%)
  between operations  0.8 us (1%)
    pallas_call x1, Pallas kernels, lanes_path(): pl.pallas_call(body, out_shape=[jax.ShapeDtypeStruct(shape, F32) for shap...  61.7 us

profile of v7, /device:TPU:0, one launch (start us, length us, event | category | flops | bytes accessed | tf_op | source)
XLA Modules:
  0.0 63.6 jit_solution(6753335918763377571)
XLA Ops:
  0.6 61.7 %shard_map.219 = (f32[2,16,32,256]{3,2,1,0:T(8,128)S(1)}, f32[8,20,128]{2,1,0:T(8,128)S(1)}, f32[8,20,128]{2,1,0:T(8,128)S(1)}) custom-call(f32[2,16,32,256]{3,2,1,0:T(8,128)} %refs_0_.1, bf16[2,256,256]{2,1,0:T(8,128)(2,1)} %constant.62.refs_1_, f32[16,32,256]{2,1,0:T(8,128)} %refs_2_.1, bf16[256,128]{1,0:T(8,128)(2,1)} %constant.43.clone.refs_3_, ...), custom_call_target="tpu_custom_call" | custom-call | tf_op jit(solution)/shard_map/pallas_call | solution.py:856
  62.3 1.1 %shard_map.220 = (f32[2,16,32,256]{3,2,1,0:T(8,128)}, f32[2,8,16,128]{3,2,1,0:T(8,128)}, f32[2,4,8,64]{3,2,1,0:T(8,128)}, f32[2,2,4,32]{3,2,1,0:T(4,128)}) custom-call(f32[2,16,32,256]{3,2,1,0:T(8,128)S(1)} %get-tuple-element.7.modulus, f32[8,20,128]{2,1,0:T(8,128)S(1)} %get-tuple-element.8.first, f32[8,20,128]{2,1,0:T(8,128)S(1)} %get-tuple-element.9.second), custom_call_target="tpu_custom_call" | custom-call | tf_op jit(solution)/shard_map/pallas_call | solution.py:870
